TPU v7x, 32 devices: a whole 2x2x4 slice. The times are simulated.
32 devices in a mesh: expert: 8 (over z, x), mp: 4 (over y, core).
Axes of the slice: x: 2, y: 2, z: 4, core: 2. Of those that a mesh axis runs over, the one named last changes fastest.
Arguments:
- tokens: bfloat16 [2048, 1024], P('expert'), may hold values from -6 to 6
- cotangent: bfloat16 [2048, 1024], P('expert'), may hold values from -6 to 6
- routes: int32 [2048, 2], P('expert'), may hold values from 0 to 7, all different within a row; in each aligned block of 256 rows (0 to 255, 256 to 511, ...) at most 96 rows name the same one
- router_weight: bfloat16 [1024, 8], replicated, may hold values from -0.1875 to 0.1875
- gate_weight: bfloat16 [8, 1024, 3584], P('expert', None, 'mp'), may hold values from -0.1875 to 0.1875
- up_weight: bfloat16 [8, 1024, 3584], P('expert', None, 'mp'), may hold values from -0.6875 to 0.6875
- down_weight: bfloat16 [8, 3584, 1024], P('expert', 'mp'), may hold values from -0.3674842 to 0.3674842
- mlp_in: float32 [3, 16], replicated, may hold values from -3.5 to 3.5
- mlp_bias: float32 [16], replicated, may hold values from -2 to 2
- mlp_out: float32 [16], replicated, may hold values from -1.5 to 1.5
Outputs:
- mixed: bfloat16 [2048, 1024], P('expert', 'mp')
- gate_update: bfloat16 [8, 1024, 3584], P('expert', None, 'mp')
- up_update: bfloat16 [8, 1024, 3584], P('expert', None, 'mp')
- down_update: bfloat16 [8, 3584, 1024], P('expert', 'mp')
- router_update: bfloat16 [1024, 8], replicated
Inputs may be any that keep to these rules, and one draw needn't show every extreme that they name: `routes`: in the rows of one index of the expert axis each expert is named at most 96 times; the two experts of a row differ.
All inputs are finite; a program needn't handle non-finite values.
Results may differ from a plain program's by a relative error of at most 0.0057.
Values may be sent and summed in bfloat16 or wider, within the bound.
A program may use at most 128 MiB of HBM per device.

v0:
```python
import jax
import jax.numpy as jnp
from jax import lax
from jax.sharding import PartitionSpec as P

D = 1024
FF = 3584


EPSILON = 1e-06


def learned_step(gradient, weight, weight_scale, grad_rms, mlp_in, mlp_bias, mlp_out):
    feat_grad = gradient / grad_rms
    feat_weight = weight.astype(jnp.float32) * weight_scale
    feat_tanh = jnp.tanh(feat_grad)
    summed = jnp.zeros_like(feat_grad)
    for neuron in range(mlp_bias.shape[0]):
        hidden = jnp.maximum(
            mlp_in[0, neuron] * feat_grad
            + mlp_in[1, neuron] * feat_weight
            + mlp_in[2, neuron] * feat_tanh
            + mlp_bias[neuron],
            0.0,
        )
        summed = summed + mlp_out[neuron] * hidden
    return summed.astype(jnp.bfloat16)


def route_tables(routes, experts, capacity):
    chosen = (routes[:, :, None] == jnp.arange(experts, dtype=jnp.int32)[None, None, :]).astype(
        jnp.int32
    )
    flat_picks = chosen.reshape(-1, experts)
    before = jnp.cumsum(flat_picks, axis=0) - flat_picks
    places = jnp.sum(before * flat_picks, axis=1).reshape(routes.shape)
    slot_hit = (places[:, :, None] == jnp.arange(capacity, dtype=jnp.int32)[None, None, :]).astype(
        jnp.bfloat16
    )
    mover = chosen.astype(jnp.bfloat16)[:, :, :, None] * slot_hit[:, :, None, :]
    return (chosen.astype(jnp.float32), mover)


def on_device(
    tokens,
    cotangent,
    routes,
    router_weight,
    gate_weight,
    up_weight,
    down_weight,
    mlp_in,
    mlp_bias,
    mlp_out,
):
    experts = lax.axis_size("expert")
    groups = lax.axis_size("mp")
    tok_count = tokens.shape[0]
    capacity = 3 * tok_count // experts
    width = tokens.shape[1]
    col_width = width // groups
    col_start = lax.axis_index("mp") * col_width
    chosen, mover = route_tables(routes, experts, capacity)
    logits = jnp.dot(tokens, router_weight, preferred_element_type=jnp.float32)
    picked = jnp.sum(logits[:, None, :] * chosen, axis=2)
    sigmas = jax.nn.sigmoid(picked)
    denominator = jnp.sum(sigmas, axis=1, keepdims=True)
    gates = sigmas / denominator
    scaled_cot = (gates[:, :, None] * cotangent.astype(jnp.float32)[:, None, :]).astype(
        jnp.bfloat16
    )
    token_cols = lax.dynamic_slice_in_dim(tokens, col_start, col_width, 1)
    cot_cols = lax.dynamic_slice_in_dim(cotangent, col_start, col_width, 1)
    send_x = jnp.einsum("tkec,td->ecd", mover, tokens, preferred_element_type=jnp.float32).astype(
        jnp.bfloat16
    )
    send_dy = jnp.einsum(
        "tkec,tkd->ecd", mover, scaled_cot, preferred_element_type=jnp.float32
    ).astype(jnp.bfloat16)
    rows_x, rows_dy = (
        lax.all_to_all(send_x, "expert", split_axis=0, concat_axis=0, tiled=True),
        lax.all_to_all(send_dy, "expert", split_axis=0, concat_axis=0, tiled=True),
    )
    rows_x = rows_x.reshape(experts * capacity, width)
    rows_dy = rows_dy.reshape(experts * capacity, width)
    w_gate = gate_weight[0]
    w_up = up_weight[0]
    w_down = down_weight[0]
    act_gate = jnp.dot(rows_x, w_gate, preferred_element_type=jnp.float32)
    act_up = jnp.dot(rows_x, w_up, preferred_element_type=jnp.float32)
    sigmoid_gate = jax.nn.sigmoid(act_gate)
    silu_gate = act_gate * sigmoid_gate
    hidden = (silu_gate * act_up).astype(jnp.bfloat16)
    partial_out = jnp.dot(hidden, w_down, preferred_element_type=jnp.float32)
    expert_sums = lax.psum_scatter(partial_out, "mp", scatter_dimension=1, tiled=True)
    back_rows = expert_sums.astype(jnp.bfloat16).reshape(experts, capacity, col_width)
    returned = lax.all_to_all(back_rows, "expert", split_axis=0, concat_axis=0, tiled=True)
    grad_down = jnp.einsum("sf,sd->fd", hidden, rows_dy, preferred_element_type=jnp.float32)
    grad_hidden = jnp.einsum("sd,fd->sf", rows_dy, w_down, preferred_element_type=jnp.float32)
    d_gate = (grad_hidden * act_up * sigmoid_gate * (1.0 + act_gate * (1.0 - sigmoid_gate))).astype(
        jnp.bfloat16
    )
    d_up = (grad_hidden * silu_gate).astype(jnp.bfloat16)
    grad_gate = jnp.einsum("sd,sf->df", rows_x, d_gate, preferred_element_type=jnp.float32)
    grad_up = jnp.einsum("sd,sf->df", rows_x, d_up, preferred_element_type=jnp.float32)
    routed = jnp.einsum("tkec,ecd->tkd", mover, returned, preferred_element_type=jnp.float32)
    mixed = (
        token_cols.astype(jnp.float32) + gates[:, 0:1] * routed[:, 0] + gates[:, 1:2] * routed[:, 1]
    ).astype(jnp.bfloat16)
    partial_dots = jnp.sum(cot_cols.astype(jnp.float32)[:, None, :] * routed, axis=2)
    gate_grads = lax.psum(partial_dots, "mp")
    mean_part = jnp.sum(gates * gate_grads, axis=1, keepdims=True)
    sigma_grads = (gate_grads - mean_part) / denominator
    logit_grads = sigma_grads * sigmas * (1.0 - sigmas)
    dense_grads = jnp.sum(logit_grads[:, :, None] * chosen, axis=1).astype(jnp.bfloat16)
    router_part = jnp.einsum("td,te->de", tokens, dense_grads, preferred_element_type=jnp.float32)
    norm_sums = lax.psum(
        (
            jnp.sum(grad_gate * grad_gate),
            jnp.sum(grad_up * grad_up),
            jnp.sum(grad_down * grad_down),
        ),
        ("expert", "mp"),
    )
    total_count = experts * width * w_gate.shape[1] * groups
    gate_rms = jnp.sqrt(norm_sums[0] / total_count + EPSILON)
    up_rms = jnp.sqrt(norm_sums[1] / total_count + EPSILON)
    down_rms = jnp.sqrt(norm_sums[2] / total_count + EPSILON)
    gate_update = learned_step(grad_gate, w_gate, D**0.5, gate_rms, mlp_in, mlp_bias, mlp_out)[None]
    up_update = learned_step(grad_up, w_up, D**0.5, up_rms, mlp_in, mlp_bias, mlp_out)[None]
    down_update = learned_step(grad_down, w_down, FF**0.5, down_rms, mlp_in, mlp_bias, mlp_out)[
        None
    ]
    router_count = width * experts
    router_grad = lax.psum(router_part, "expert")
    router_rms = jnp.sqrt(jnp.sum(router_grad * router_grad) / router_count + EPSILON)
    router_update = learned_step(
        router_grad, router_weight, D**0.5, router_rms, mlp_in, mlp_bias, mlp_out
    )
    return (mixed, gate_update, up_update, down_update, router_update)


def solution(mesh):
    placed = (
        P("expert", None),
        P("expert", None),
        P("expert", None),
        P(),
        P("expert", None, "mp"),
        P("expert", None, "mp"),
        P("expert", "mp", None),
        P(),
        P(),
        P(),
    )
    return jax.shard_map(
        on_device,
        mesh=mesh,
        in_specs=placed,
        out_specs=(
            P("expert", "mp"),
            P("expert", None, "mp"),
            P("expert", None, "mp"),
            P("expert", "mp", None),
            P(),
        ),
        check_vma=False,
    )
```

profile of v0, /device:TPU:0, one launch (start us, length us, event | category | flops | bytes accessed | tf_op | source)
XLA Modules:
  0.0 487.7 jit_solution(184797794823028223)
XLA Ops:
  7.2 0.0 copy-start
  7.2 0.0 reduce-scatter.2.cloned.1.call-start
  7.2 1.0 copy.27
  8.2 0.1 eq.62
  8.3 0.1 eq.58
  8.5 0.7 fusion.423
  9.2 1.1 reduce-window.6
  10.4 0.2 slice_reduce_fusion
  10.6 0.1 fusion.422
  10.7 0.1 eq.66
  10.9 0.1 copy.29
  11.0 0.1 convert_reduce_fusion
  11.1 0.6 convolution_convert_fusion
  11.7 44.1 %all_to_all.15 = bf16[8,96,1024]{2,1,0:T(8,128)(2,1)S(1)} all-to-all(bf16[8,96,1024]{2,1,0:T(8,128)(2,1)S(1)} %convolution_convert_fusion), channel_id=1, replica_groups=mesh['expert'=8,'mp'=4] {'expert'}, dimensions={0} | all-to-all | bytes 3145728 | tf_op jit(solution)/shard_map/all_to_all | solution.py:81
  55.8 1.8 fusion.295
  57.6 0.3 copy-done.4
  57.9 3.5 multiply_convert_fusion.2
  61.3 1.1 copy-done.22
  62.4 0.0 copy-done.6
  62.4 3.5 fusion.291
  65.9 0.0 reduce-scatter.2.cloned.1.call-update
  65.9 1.1 convert_element_type.106
  67.0 35.8 %reduce-scatter.2.cloned.1.call-done = f32[768,256]{1,0:T(8,128)} async-done(((f32[768,1024]{1,0:T(8,128)}), f32[768,256]{1,0:T(8,128)}) %reduce-scatter.2.cloned.1.call-update) | async-done | bytes 786448 | tf_op jit(solution)/shard_map/reduce_scatter | solution.py:95
  102.8 1.9 convert_element_type.104
  104.7 5.5 %all-to-all-start.1 = ((bf16[8,96,256]{2,1,0:T(8,128)(2,1)}), bf16[8,96,256]{2,1,0:T(8,128)(2,1)}, u32[]{:S(2)}, u32[]{:S(2)}) async-start(bf16[8,96,256]{2,1,0:T(8,128)(2,1)} %bitcast.8), calls=%async_computation.2 | async-start | bytes 786432 | tf_op jit(solution)/shard_map/all_to_all | solution.py:97
  110.2 1.6 dynamic-slice_convert_fusion
  111.8 1.8 copy.30
  113.6 0.0 copy-done.14
  113.6 0.2 fusion.436
  113.9 0.6 fusion.429
  114.5 7.4 %all-to-all-done.1 = bf16[8,96,256]{2,1,0:T(8,128)(2,1)} async-done(((bf16[8,96,256]{2,1,0:T(8,128)(2,1)}), bf16[8,96,256]{2,1,0:T(8,128)(2,1)}, u32[]{:S(2)}, u32[]{:S(2)}) %all-to-all-start.1) | async-done | bytes 393248 | tf_op jit(solution)/shard_map/all_to_all | solution.py:97
  121.9 2.3 multiply_reduce_fusion.3
  124.2 5.9 %psum.38 = f32[256,2]{0,1:T(2,128)S(1)} all-reduce(f32[256,2]{0,1:T(2,128)S(1)} %get-tuple-element.111), channel_id=1, replica_groups=mesh['expert'=8,'mp'=4] {'mp'}, use_global_device_ids=true, to_apply=%region_14.15 | all-reduce | flops 512 | bytes 4096 | tf_op jit(solution)/shard_map/psum | solution.py:111
  130.1 0.6 multiply_reduce_fusion.7
  130.6 0.6 copy-done.17
  131.2 2.2 bitcast_convert_fusion
  133.4 4.4 all-to-all-start.2
  137.9 0.7 fusion.432
  139.2 0.7 fusion.430
  148.3 0.7 fusion.431
  160.0 0.1 copy.34
  160.1 0.0 copy-done.12
  160.1 0.7 fusion.435
  160.8 0.7 fusion.434
  161.5 0.0 copy-done.18
  161.6 0.1 fusion.321
  161.6 0.8 copy.31
  162.4 0.2 convolution_bitcast_fusion
  162.6 37.5 %psum.39 = f32[1024,8]{0,1:T(8,128)S(1)} all-reduce(f32[1024,8]{0,1:T(8,128)S(1)} %convolution_bitcast_fusion), channel_id=1, replica_groups=mesh['expert'=8,'mp'=4] {'expert'}, use_global_device_ids=true, to_apply=%region_17.18 | all-reduce | flops 8192 | bytes 65536 | tf_op jit(solution)/shard_map/psum | solution.py:135
  200.2 0.6 multiply_reduce_fusion.4
  201.5 40.7 %fusion.420 = bf16[1024,8]{0,1:T(8,128)(2,1)} fusion(bf16[1024,8]{0,1:T(8,128)(2,1)S(1)} %copy-done.14, f32[1024,8]{0,1:T(8,128)S(1)} %psum.39, f32[]{:T(128)} %bitcast.98, f32[]{:T(128)} %bitcast.97, f32[]{:T(128)} %bitcast.96, f32[]{:T(128)} %bitcast.95, f32[]{:T(128)} %bitcast.94, f32[]{:T(128)} %bitcast.93, f32[]{:T(128)} %bitcast.92, f32[]{:T(128)} %bitcast.91, ...), kind=kLoop, calls=%fused_computation.530 | loop fusion | flops 1196032 | bytes 65860 | tf_op jit(solution)/shard_map/convert_element_type | solution.py:27
  242.2 0.0 all-to-all-done.2
  242.2 3.9 fusion.289
  246.1 0.0 copy-start.9
  246.1 5.6 %multiply_reduce_fusion = (f32[]{:T(128)}, f32[896,1024]{1,0:T(8,128)}) fusion(bf16[768,896]{1,0:T(8,128)(2,1)S(1)} %copy-done.23, bf16[768,1024]{1,0:T(8,128)(2,1)} %bitcast.20), kind=kOutput, calls=%fused_computation.341 | convolution fusion | flops 1411121152 | bytes 6619140 | tf_op jit(solution)/shard_map/sf,sd->fd/dot_general | solution.py:98
  251.7 4.5 multiply_reduce_fusion.1
  256.2 4.7 multiply_reduce_fusion.2
  261.0 37.3 %all-reduce = (f32[]{:T(128)}, f32[]{:T(128)}, f32[]{:T(128)}) all-reduce(f32[]{:T(128)} %get-tuple-element.113, f32[]{:T(128)} %get-tuple-element.115, f32[]{:T(128)} %get-tuple-element.117), channel_id=1, replica_groups=mesh['expert'=8,'mp'=4] {'expert','mp'}, use_global_device_ids=true, to_apply=%region_8.9 | all-reduce | flops 3 | bytes 24 | tf_op jit(solution)/shard_map/psum | solution.py:117
  300.4 0.0 copy-start.5
  300.4 61.0 %fusion.297 = bf16[1,1024,896]{2,1,0:T(8,128)(2,1)} fusion(f32[]{:T(128)} %bitcast.98, f32[]{:T(128)} %bitcast.97, f32[]{:T(128)} %bitcast.96, f32[]{:T(128)} %bitcast.95, f32[]{:T(128)} %bitcast.94, f32[]{:T(128)} %bitcast.93, f32[]{:T(128)} %bitcast.92, f32[]{:T(128)} %bitcast.91, f32[]{:T(128)} %bitcast.90, f32[]{:T(128)} %bitcast.89, f32[]{:T(128)} %bitcast.88, ...), kind=kLoop, calls=%fused_computation.378 | loop fusion | flops 133955584 | bytes 7340356 | tf_op jit(solution)/shard_map/broadcast_in_dim | solution.py:129
  361.4 0.0 copy-start.7
  361.4 60.1 %fusion.298 = bf16[1,1024,896]{2,1,0:T(8,128)(2,1)} fusion(f32[]{:T(128)} %bitcast.98, f32[]{:T(128)} %bitcast.97, f32[]{:T(128)} %bitcast.96, f32[]{:T(128)} %bitcast.95, f32[]{:T(128)} %bitcast.94, f32[]{:T(128)} %bitcast.93, f32[]{:T(128)} %bitcast.92, f32[]{:T(128)} %bitcast.91, f32[]{:T(128)} %bitcast.90, f32[]{:T(128)} %bitcast.89, f32[]{:T(128)} %bitcast.88, ...), kind=kLoop, calls=%fused_computation.379 | loop fusion | flops 133955584 | bytes 7340356 | tf_op jit(solution)/shard_map/broadcast_in_dim | solution.py:130
  421.6 0.0 copy-done.7
  421.6 59.3 %fusion.299 = bf16[1,896,1024]{2,1,0:T(8,128)(2,1)} fusion(f32[]{:T(128)} %bitcast.98, f32[]{:T(128)} %bitcast.97, f32[]{:T(128)} %bitcast.116, f32[]{:T(128)} %bitcast.95, f32[]{:T(128)} %bitcast.94, f32[]{:T(128)} %bitcast.93, f32[]{:T(128)} %bitcast.92, f32[]{:T(128)} %bitcast.115, f32[]{:T(128)} %bitcast.90, f32[]{:T(128)} %bitcast.89, f32[]{:T(128)} %bitcast.88, ...), kind=kLoop, calls=%fused_computation.380 | loop fusion | flops 133955584 | bytes 7340356 | tf_op jit(solution)/shard_map/broadcast_in_dim | solution.py:131
  (47 shorter events, 0.3 us)
Async XLA Ops:
  7.2 3.9 copy-start
  7.2 48.6 %copy-start.3 = (bf16[1,1024,896]{2,1,0:T(8,128)(2,1)S(1)}, bf16[1,1024,896]{2,1,0:T(8,128)(2,1)}, u32[]{:S(2)}) copy-start(bf16[1,1024,896]{2,1,0:T(8,128)(2,1)} %param.14) | copy-start | bytes 5505028
  7.2 95.6 %reduce-scatter.2.cloned.1.call-start = ((), (), s32[]{:S(2)}) async-start(), calls=%async_computation.4 | async-start | bytes 3932160 | tf_op jit(solution)/shard_map/reduce_scatter | solution.py:95
  55.8 1.8 copy-start.8
  55.8 2.1 copy-start.4
  57.9 3.5 copy-start.20
  57.9 4.5 copy-start.6
  61.3 1.1 copy-start.22
  65.8 47.8 %copy-start.14 = (bf16[1024,8]{0,1:T(8,128)(2,1)S(1)}, bf16[1024,8]{0,1:T(8,128)(2,1)}, u32[]{:S(2)}) copy-start(bf16[1024,8]{0,1:T(8,128)(2,1)} %param.13) | copy-start | bytes 49156
  65.9 48.0 %copy-start.15 = (s32[256,2]{0,1:T(2,128)S(1)}, s32[256,2]{0,1:T(2,128)}, u32[]{:S(2)}) copy-start(s32[256,2]{0,1:T(2,128)} %param.12) | copy-start | bytes 6148
  104.7 17.2 %all-to-all-start.1 = ((bf16[8,96,256]{2,1,0:T(8,128)(2,1)}), bf16[8,96,256]{2,1,0:T(8,128)(2,1)}, u32[]{:S(2)}, u32[]{:S(2)}) async-start(bf16[8,96,256]{2,1,0:T(8,128)(2,1)} %bitcast.8), calls=%async_computation.2 | async-start | bytes 786432 | tf_op jit(solution)/shard_map/all_to_all | solution.py:97
  130.6 0.6 copy-start.17
  131.2 6.7 %copy-start.11 = (f32[3,16]{1,0:T(4,128)S(1)}, f32[3,16]{1,0:T(4,128)}, u32[]{:S(2)}) copy-start(f32[3,16]{1,0:T(4,128)} %param.17) | copy-start | bytes 580
  131.2 28.9 %copy-start.12 = (f32[16]{0:T(128)S(1)}, f32[16]{0:T(128)}, u32[]{:S(2)}) copy-start(f32[16]{0:T(128)} %param.18) | copy-start | bytes 196
  131.2 29.6 %copy-start.13 = (f32[16]{0:T(128)S(1)}, f32[16]{0:T(128)}, u32[]{:S(2)}) copy-start(f32[16]{0:T(128)} %param.19) | copy-start | bytes 196
  133.4 28.1 %copy-start.18 = (f32[256,2]{0,1:T(2,128)S(1)}, f32[256,2]{0,1:T(2,128)}, u32[]{:S(2)}) copy-start(f32[256,2]{0,1:T(2,128)} %copy-done.17) | copy-start | bytes 6148
  133.4 28.1 %copy-start.10 = (f32[256,2,256]{0,2,1:T(8,128)S(1)}, f32[256,2,256]{0,2,1:T(8,128)}, u32[]{:S(2)}) copy-start(f32[256,2,256]{0,2,1:T(8,128)} %get-tuple-element.112) | copy-start | bytes 1572868
  133.4 29.0 %copy-start.16 = (f32[256,2]{0,1:T(2,128)S(1)}, f32[256,2]{0,1:T(2,128)}, u32[]{:S(2)}) copy-start(f32[256,2]{0,1:T(2,128)} %get-tuple-element.26) | copy-start | bytes 6148
  133.4 29.0 %copy-start.19 = (f32[256]{0:T(256)S(1)}, f32[256]{0:T(256)}, u32[]{:S(2)}) copy-start(f32[256]{0:T(256)} %get-tuple-element.23) | copy-start | bytes 3076
  133.4 108.7 %all-to-all-start.2 = ((bf16[8,96,1024]{2,1,0:T(8,128)(2,1)}), bf16[8,96,1024]{2,1,0:T(8,128)(2,1)}, u32[]{:S(2)}, u32[]{:S(2)}) async-start(bf16[8,96,1024]{2,1,0:T(8,128)(2,1)} %bitcast_convert_fusion), calls=%async_computation.3 | async-start | bytes 3145728 | tf_op jit(solution)/shard_map/all_to_all | solution.py:82
  242.2 3.9 copy-start.23
  246.1 5.6 %copy-start.9 = (bf16[8,96,1024]{2,1,0:T(8,128)(2,1)S(1)}, bf16[8,96,1024]{2,1,0:T(8,128)(2,1)}, u32[]{:S(2)}) copy-start(bf16[8,96,1024]{2,1,0:T(8,128)(2,1)} %copy-done.8) | copy-start | bytes 4718596
  246.1 5.6 %copy-start.21 = (f32[768,896]{1,0:T(8,128)S(1)}, f32[768,896]{1,0:T(8,128)}, u32[]{:S(2)}) copy-start(f32[768,896]{1,0:T(8,128)} %copy-done.20) | copy-start | bytes 8257540
  251.7 4.5 copy-start.24
  300.4 61.0 %copy-start.2 = (f32[1024,896]{1,0:T(8,128)S(1)}, f32[1024,896]{1,0:T(8,128)}, u32[]{:S(2)}) copy-start(f32[1024,896]{1,0:T(8,128)} %get-tuple-element.116) | copy-start | bytes 11010052
  300.4 61.0 %copy-start.5 = (bf16[1,1024,896]{2,1,0:T(8,128)(2,1)S(1)}, bf16[1,1024,896]{2,1,0:T(8,128)(2,1)}, u32[]{:S(2)}) copy-start(bf16[1,1024,896]{2,1,0:T(8,128)(2,1)} %param.15) | copy-start | bytes 5505028
  361.4 60.1 %copy-start.1 = (f32[896,1024]{1,0:T(8,128)S(1)}, f32[896,1024]{1,0:T(8,128)}, u32[]{:S(2)}) copy-start(f32[896,1024]{1,0:T(8,128)} %get-tuple-element.118) | copy-start | bytes 11010052
  361.4 60.1 %copy-start.7 = (bf16[1,896,1024]{2,1,0:T(8,128)(2,1)S(1)}, bf16[1,896,1024]{2,1,0:T(8,128)(2,1)}, u32[]{:S(2)}) copy-start(bf16[1,896,1024]{2,1,0:T(8,128)(2,1)} %param.16) | copy-start | bytes 5505028
Sparse Core Ops, SparseCore 0:
  66.0 36.7 reduce-scatter.1
where the time goes:
time: 492 us; the launch traced here: 488 us
  other arithmetic  230 us (47%)
  blocking collectives  125 us (25%)
  waiting for transfers between devices  43.2 us (9%)
  between operations  37 us (8%)
  matrix products  32.9 us (7%)
  starting transfers between devices  9.97 us (2%)
  local copies, waits for them, and re-layouts  9.91 us (2%)
    broadcast_in_dim x1, other arithmetic, on_device(): learned_step(grad_gate, w_gate, D ** 0.5, gate_rms, mlp_in, mlp_bias, mlp...  61 us
    broadcast_in_dim x1, other arithmetic, on_device(): learned_step(grad_up, w_up, D ** 0.5, up_rms, mlp_in, mlp_bias, mlp_out)  60.1 us
    broadcast_in_dim x1, other arithmetic, on_device(): learned_step(grad_down, w_down, FF ** 0.5, down_rms, mlp_in, mlp_bias, ml...  59.3 us
    all_to_all x1, blocking collectives, on_device(): lax.all_to_all(send_x, 'expert', split_axis=0, concat_axis=0, tiled=True)  44.1 us
    convert_element_type x1, other arithmetic, learned_step(): return summed.astype(jnp.bfloat16)  40.7 us
    psum x1, blocking collectives, on_device(): router_grad = lax.psum(router_part, 'expert')  37.5 us
    psum x1, blocking collectives, on_device(): lax.psum((jnp.sum(grad_gate * grad_gate), jnp.sum(grad_up * grad_up), jnp...  37.3 us
    reduce_scatter x1, waiting for transfers between devices, on_device(): lax.psum_scatter(partial_out, 'mp', scatter_dimension=1, tiled=True)  35.8 us
  transfers between devices with their start and end apart: 3, of which 2 were waited for; matrix products, arithmetic and copies ran while one was open for 11% of the time, Pallas kernels for 0%

commit v1 on v0

v1 whole, which is shorter than its diff:
```python
import functools

import jax
import jax.numpy as jnp
from jax import lax
from jax.experimental import pallas as pl
from jax.experimental.pallas import tpu as pltpu
from jax.sharding import PartitionSpec as P

EPSILON = 1e-06
MESH = pl.DeviceIdType.MESH


def dispatch_kernel(n, groups, colw, send_ref, out_ref, loc, s1, r1, ls, lr, hs, hr, fs, fr):
    me = lax.axis_index("expert")
    col = lax.axis_index("mp")
    partner = col + 1 - 2 * lax.rem(col, 2)
    highs = groups // 2
    barrier = pltpu.get_barrier_semaphore()

    def greet(i, _):
        pl.semaphore_signal(
            barrier, inc=1, device_id=(lax.rem(me + i, n), col), device_id_type=MESH
        )
        return 0

    lax.fori_loop(1, n, greet, 0)
    pl.semaphore_signal(barrier, inc=1, device_id=(me, partner), device_id_type=MESH)
    for h in range(1, highs):
        pl.semaphore_signal(
            barrier, inc=1, device_id=(me, lax.rem(col + 2 * h, groups)), device_id_type=MESH
        )
    pl.semaphore_wait(barrier, n - 1 + 1 + highs - 1)

    def cols(c):
        return pl.ds(pl.multiple_of(c * colw, 128), colw)

    def spread(i):
        peer = lax.rem(me + i, n)
        return pltpu.make_async_remote_copy(
            src_ref=send_ref.at[:, peer],
            dst_ref=out_ref.at[:, me, :, cols(col)],
            send_sem=s1.at[i],
            recv_sem=r1.at[i],
            device_id=(peer, col),
            device_id_type=MESH,
        )

    def block(owner, i):
        return out_ref.at[:, lax.rem(me - i + n, n), :, cols(owner)]

    def to(owner, i, send, recv, target):
        ref = block(owner, i)
        return pltpu.make_async_remote_copy(
            src_ref=ref,
            dst_ref=ref,
            send_sem=send,
            recv_sem=recv,
            device_id=(me, target),
            device_id_type=MESH,
        )

    def low(i):
        return to(col, i, ls.at[i], lr.at[i], partner)

    def high(h, i):
        return to(col, i, hs.at[h - 1, i], hr.at[h - 1, i], lax.rem(col + 2 * h, groups))

    def forward(h, i):
        owner = lax.rem(col - 2 * h + 2 * groups, groups)
        return to(owner, i, fs.at[h - 1, i], fr.at[h - 1, i], partner)

    own = pltpu.make_async_copy(send_ref.at[:, me], out_ref.at[:, me, :, cols(col)], loc)
    own.start()

    def start(i, _):
        spread(i).start()
        return 0

    lax.fori_loop(1, n, start, 0)
    own.wait()

    def share(i):
        for h in range(1, highs):
            high(h, i).start()
        low(i).start()

    def relay(i):
        for h in range(1, highs):
            high(h, i).wait_recv()
            forward(h, i).start()

    share(0)

    def step(i, _):
        spread(i).wait_recv()
        share(i)
        relay(i - 1)
        return 0

    lax.fori_loop(1, n, step, 0)
    relay(n - 1)

    def finish(i, _):
        low(i).wait()
        for h in range(1, highs):
            high(h, i).wait_send()
            forward(h, i).wait()
        return 0

    def finish_spread(i, _):
        spread(i).wait_send()
        return 0

    lax.fori_loop(0, n, finish, 0)
    lax.fori_loop(1, n, finish_spread, 0)


def dispatch(send, n, groups):
    _, _, cap, colw = send.shape
    dma = pltpu.SemaphoreType.DMA
    highs = max(groups // 2 - 1, 1)
    return pl.pallas_call(
        functools.partial(dispatch_kernel, n, groups, colw),
        out_shape=jax.ShapeDtypeStruct((2, n, cap, colw * groups), send.dtype),
        in_specs=[pl.BlockSpec(memory_space=pltpu.VMEM)],
        out_specs=pl.BlockSpec(memory_space=pltpu.VMEM),
        scratch_shapes=[
            dma,
            dma((n,)),
            dma((n,)),
            dma((n,)),
            dma((n,)),
            dma((highs, n)),
            dma((highs, n)),
            dma((highs, n)),
            dma((highs, n)),
        ],
        compiler_params=pltpu.CompilerParams(collective_id=0, has_side_effects=True),
        name="dispatch",
    )(send)


def gather_all_kernel(n, groups, x_ref, out_ref, loc, ss, rs):
    total = n * groups
    me = lax.axis_index("expert") * groups + lax.axis_index("mp")
    barrier = pltpu.get_barrier_semaphore()

    def place(i):
        peer = lax.rem(me + i, total)
        return (peer // groups, lax.rem(peer, groups))

    def greet(i, _):
        pl.semaphore_signal(barrier, inc=1, device_id=place(i), device_id_type=MESH)
        return 0

    own = pltpu.make_async_copy(x_ref, out_ref.at[me], loc)
    own.start()
    lax.fori_loop(1, total, greet, 0)
    pl.semaphore_wait(barrier, total - 1)

    def copy(i):
        return pltpu.make_async_remote_copy(
            src_ref=x_ref,
            dst_ref=out_ref.at[me],
            send_sem=ss.at[i],
            recv_sem=rs.at[i],
            device_id=place(i),
            device_id_type=MESH,
        )

    def start(i, _):
        copy(i).start()
        return 0

    def finish(i, _):
        copy(i).wait()
        return 0

    lax.fori_loop(1, total, start, 0)
    own.wait()
    lax.fori_loop(1, total, finish, 0)


def gather_all(x, n, groups):
    total = n * groups
    return pl.pallas_call(
        functools.partial(gather_all_kernel, n, groups),
        out_shape=jax.ShapeDtypeStruct((total,) + x.shape, x.dtype),
        in_specs=[pl.BlockSpec(memory_space=pltpu.VMEM)],
        out_specs=pl.BlockSpec(memory_space=pltpu.VMEM),
        scratch_shapes=[
            pltpu.SemaphoreType.DMA,
            pltpu.SemaphoreType.DMA((total,)),
            pltpu.SemaphoreType.DMA((total,)),
        ],
        compiler_params=pltpu.CompilerParams(collective_id=1, has_side_effects=True),
        name="gather_all",
    )(x)


def gather_experts_kernel(n, x_ref, out_ref, buf, loc, ss, rs):
    me = lax.axis_index("expert")
    col = lax.axis_index("mp")
    barrier = pltpu.get_barrier_semaphore()

    def greet(i, _):
        pl.semaphore_signal(
            barrier, inc=1, device_id=(lax.rem(me + i, n), col), device_id_type=MESH
        )
        return 0

    own = pltpu.make_async_copy(x_ref, buf.at[me], loc)
    own.start()
    lax.fori_loop(1, n, greet, 0)
    pl.semaphore_wait(barrier, n - 1)

    def copy(i):
        return pltpu.make_async_remote_copy(
            src_ref=x_ref,
            dst_ref=buf.at[me],
            send_sem=ss.at[i],
            recv_sem=rs.at[i],
            device_id=(lax.rem(me + i, n), col),
            device_id_type=MESH,
        )

    def start(i, _):
        copy(i).start()
        return 0

    def finish(i, _):
        copy(i).wait()
        return 0

    lax.fori_loop(1, n, start, 0)
    own.wait()
    lax.fori_loop(1, n, finish, 0)
    out_ref[...] = buf[0]

    def add(i, _):
        out_ref[...] += buf[i]
        return 0

    lax.fori_loop(1, n, add, 0)


def sum_experts(x, n):
    return pl.pallas_call(
        functools.partial(gather_experts_kernel, n),
        out_shape=jax.ShapeDtypeStruct(x.shape, x.dtype),
        in_specs=[pl.BlockSpec(memory_space=pltpu.VMEM)],
        out_specs=pl.BlockSpec(memory_space=pltpu.VMEM),
        scratch_shapes=[
            pltpu.VMEM((n,) + x.shape, x.dtype),
            pltpu.SemaphoreType.DMA,
            pltpu.SemaphoreType.DMA((n,)),
            pltpu.SemaphoreType.DMA((n,)),
        ],
        compiler_params=pltpu.CompilerParams(collective_id=2, has_side_effects=True),
        name="sum_experts",
    )(x)


def update_kernel(units, chunk, coef_ref, g_ref, w_ref, out_ref):
    rows, width = g_ref.shape
    strips = width // 128

    def body(step, _):
        r = pl.ds(pl.multiple_of((step // strips) * chunk, chunk), chunk)
        c = pl.ds(pl.multiple_of(lax.rem(step, strips) * 128, 128), 128)

        def coef(i):
            return jnp.concatenate([coef_ref[i]] * (chunk // 8), axis=0)

        f0 = g_ref[r, c] * coef(5 * units)
        f1 = w_ref[r, c].astype(jnp.float32)
        f2 = jnp.tanh(f0)
        acc = coef(5 * units + 1)
        for j in range(units):
            y = coef(j) * f0 + coef(units + j) * f1 + coef(2 * units + j) * f2
            acc = acc + coef(4 * units + j) * jnp.maximum(y, coef(3 * units + j))
        out_ref[r, c] = acc.astype(jnp.bfloat16)
        return 0

    lax.fori_loop(0, (rows // chunk) * strips, body, 0)


def update(g, w, scale, rms, mlp_in, mlp_bias, mlp_out):
    units = mlp_bias.shape[0]
    table = jnp.concatenate(
        [
            mlp_in[0],
            mlp_in[1] * scale,
            mlp_in[2],
            -mlp_bias,
            mlp_out,
            (1.0 / rms)[None],
            jnp.sum(mlp_out * mlp_bias)[None],
        ]
    )
    table = jnp.broadcast_to(table[:, None, None], (table.shape[0], 8, 128))
    rows, width = g.shape
    chunk = 64 if rows % 64 == 0 else rows
    steps = 4 if rows % (4 * chunk) == 0 else 2 if rows % (2 * chunk) == 0 else 1
    if chunk < 64:
        chunk = 8
    block = rows // steps
    return pl.pallas_call(
        functools.partial(update_kernel, units, chunk),
        grid=(steps,),
        out_shape=jax.ShapeDtypeStruct((rows, width), jnp.bfloat16),
        in_specs=[
            pl.BlockSpec(table.shape, lambda i: (0, 0, 0)),
            pl.BlockSpec((block, width), lambda i: (i, 0)),
            pl.BlockSpec((block, width), lambda i: (i, 0)),
        ],
        out_specs=pl.BlockSpec((block, width), lambda i: (i, 0)),
        cost_estimate=pl.CostEstimate(
            flops=rows * width * 9 * units, bytes_accessed=rows * width * 8, transcendentals=rows * width
        ),
        name="update",
    )(table, g, w)


def route_tables(routes, experts, capacity):
    chosen = (routes[:, :, None] == jnp.arange(experts, dtype=jnp.int32)[None, None, :]).astype(
        jnp.int32
    )
    flat_picks = chosen.reshape(-1, experts)
    before = jnp.cumsum(flat_picks, axis=0) - flat_picks
    places = jnp.sum(before * flat_picks, axis=1).reshape(routes.shape)
    slot_hit = (places[:, :, None] == jnp.arange(capacity, dtype=jnp.int32)[None, None, :]).astype(
        jnp.bfloat16
    )
    mover = chosen.astype(jnp.bfloat16)[:, :, :, None] * slot_hit[:, :, None, :]
    return (chosen.astype(jnp.float32), mover)


def on_device(
    tokens,
    cotangent,
    routes,
    router_weight,
    gate_weight,
    up_weight,
    down_weight,
    mlp_in,
    mlp_bias,
    mlp_out,
):
    experts = lax.axis_size("expert")
    groups = lax.axis_size("mp")
    tok_count = tokens.shape[0]
    capacity = 3 * tok_count // experts
    width = tokens.shape[1]
    col_width = width // groups
    mp = lax.axis_index("mp")
    me = lax.axis_index("expert")
    col_start = mp * col_width
    chosen, mover = route_tables(routes, experts, capacity)
    logits = jnp.dot(tokens, router_weight, preferred_element_type=jnp.float32)
    picked = jnp.sum(logits[:, None, :] * chosen, axis=2)
    sigmas = jax.nn.sigmoid(picked)
    denominator = jnp.sum(sigmas, axis=1, keepdims=True)
    gates = sigmas / denominator
    token_cols = lax.dynamic_slice_in_dim(tokens, col_start, col_width, 1)
    cot_cols = lax.dynamic_slice_in_dim(cotangent, col_start, col_width, 1)
    scaled_cot = (gates[:, :, None] * cot_cols.astype(jnp.float32)[:, None, :]).astype(
        jnp.bfloat16
    )
    send_x = jnp.einsum(
        "tkec,td->ecd", mover, token_cols, preferred_element_type=jnp.float32
    ).astype(jnp.bfloat16)
    send_dy = jnp.einsum(
        "tkec,tkd->ecd", mover, scaled_cot, preferred_element_type=jnp.float32
    ).astype(jnp.bfloat16)
    got = dispatch(jnp.stack([send_x, send_dy]), experts, groups)
    slots = experts * capacity
    rows_x = got[0].reshape(slots, width)
    rows_dy = got[1].reshape(slots, width)
    w_gate = gate_weight[0]
    w_up = up_weight[0]
    w_down = down_weight[0]
    hidden_units = w_gate.shape[1] * groups
    act_gate = jnp.dot(rows_x, w_gate, preferred_element_type=jnp.float32)
    act_up = jnp.dot(rows_x, w_up, preferred_element_type=jnp.float32)
    sigmoid_gate = jax.nn.sigmoid(act_gate)
    silu_gate = act_gate * sigmoid_gate
    hidden = (silu_gate * act_up).astype(jnp.bfloat16)
    partial_out = jnp.dot(hidden, w_down, preferred_element_type=jnp.float32).astype(jnp.bfloat16)
    total_out = lax.dynamic_slice_in_dim(partial_out, col_start, col_width, 1).astype(jnp.float32)
    for shift in range(1, groups):
        target = lax.rem(mp + shift, groups)
        piece = lax.dynamic_slice_in_dim(partial_out, target * col_width, col_width, 1)
        moved = lax.ppermute(piece, "mp", [(m, (m + shift) % groups) for m in range(groups)])
        total_out = total_out + moved.astype(jnp.float32)
    back_rows = total_out.astype(jnp.bfloat16).reshape(experts, capacity, col_width)
    returned = lax.all_to_all(back_rows, "expert", split_axis=0, concat_axis=0, tiled=True)

    grad_down = jnp.einsum("sf,sd->fd", hidden, rows_dy, preferred_element_type=jnp.float32)
    grad_hidden = jnp.einsum("sd,fd->sf", rows_dy, w_down, preferred_element_type=jnp.float32)
    d_gate = (grad_hidden * act_up * sigmoid_gate * (1.0 + act_gate * (1.0 - sigmoid_gate))).astype(
        jnp.bfloat16
    )
    d_up = (grad_hidden * silu_gate).astype(jnp.bfloat16)
    inner = jnp.sum(grad_hidden * hidden.astype(jnp.float32), axis=1)
    grad_gate = jnp.einsum("sd,sf->df", rows_x, d_gate, preferred_element_type=jnp.float32)
    grad_up = jnp.einsum("sd,sf->df", rows_x, d_up, preferred_element_type=jnp.float32)

    norms = jnp.stack(
        [
            jnp.sum(grad_gate * grad_gate),
            jnp.sum(grad_up * grad_up),
            jnp.sum(grad_down * grad_down),
        ]
    )
    need = slots + 3
    lines = -(-need // 1024) * 8
    parcel = jnp.concatenate([inner, norms, jnp.zeros((lines * 128 - need,), jnp.float32)])
    parcels = gather_all(parcel.reshape(lines, 128), experts, groups)
    parcels = jnp.sum(parcels.reshape(experts, groups, lines * 128), axis=1)
    norm_sums = jnp.sum(parcels[:, slots : slots + 3], axis=0)
    inner_own = lax.dynamic_slice(parcels, (0, me * capacity), (experts, capacity))

    total_count = experts * width * hidden_units
    rms = jnp.sqrt(norm_sums / total_count + EPSILON)
    net = (mlp_in, mlp_bias, mlp_out)
    gate_update = update(grad_gate, w_gate, width**0.5, rms[0], *net)[None]
    up_update = update(grad_up, w_up, width**0.5, rms[1], *net)[None]
    down_update = update(grad_down, w_down, hidden_units**0.5, rms[2], *net)[None]

    gated = jnp.sum(mover.astype(jnp.float32) * inner_own[None, None], axis=(2, 3))
    logit_grads = (gated - gates * jnp.sum(gated, axis=1, keepdims=True)) * (1.0 - sigmas)
    dense_grads = jnp.sum(logit_grads[:, :, None] * chosen, axis=1).astype(jnp.bfloat16)
    router_part = jnp.einsum("te,td->ed", dense_grads, tokens, preferred_element_type=jnp.float32)
    router_grad = sum_experts(router_part, experts)
    router_rms = jnp.sqrt(jnp.sum(router_grad * router_grad) / (width * experts) + EPSILON)
    router_update = update(router_grad, router_weight.T, width**0.5, router_rms, *net).T

    routed = jnp.einsum("tkec,ecd->tkd", mover, returned, preferred_element_type=jnp.float32)
    mixed = (
        token_cols.astype(jnp.float32) + gates[:, 0:1] * routed[:, 0] + gates[:, 1:2] * routed[:, 1]
    ).astype(jnp.bfloat16)
    return (mixed, gate_update, up_update, down_update, router_update)


def solution(mesh):
    placed = (
        P("expert", None),
        P("expert", None),
        P("expert", None),
        P(),
        P("expert", None, "mp"),
        P("expert", None, "mp"),
        P("expert", "mp", None),
        P(),
        P(),
        P(),
    )
    return jax.shard_map(
        on_device,
        mesh=mesh,
        in_specs=placed,
        out_specs=(
            P("expert", "mp"),
            P("expert", None, "mp"),
            P("expert", None, "mp"),
            P("expert", "mp", None),
            P(),
        ),
        check_vma=False,
    )
```

time: 492 us -> 204 us (0.41)
  other arithmetic: 230 us -> 12.2 us
  Pallas kernels: 0 us -> 131 us
  blocking collectives: 125 us -> 0 us
  waiting for transfers between devices: 43.2 us -> 0.01 us
  between operations: 37 us -> 3.71 us
  local copies, waits for them, and re-layouts: 9.91 us -> 18.6 us
    broadcast_in_dim x3 -> x0, other arithmetic: 180 us -> none  [the longest x1 61 us: on_device(): learned_step(grad_gate, w_gate, D ** 0.5, gate_rms, mlp_in, mlp_bias, mlp...]
    pallas_call x0 -> x7, Pallas kernels: none -> 131 us  [the longest x4 65.2 us: update(): pl.pallas_call(functools.partial(update_kernel, units, chunk), grid=(step...]
    psum x3 -> x0, blocking collectives: 80.8 us -> none  [the longest x1 37.5 us: on_device(): router_grad = lax.psum(router_part, 'expert')]
    all_to_all x1 -> x0, blocking collectives: 44.1 us -> none  [on_device(): lax.all_to_all(send_x, 'expert', split_axis=0, concat_axis=0, tiled=True)]
    convert_element_type x4 -> x2, other arithmetic: 45.4 us -> 3.12 us  [the longest x1 2.19 us: on_device(): total_out.astype(jnp.bfloat16).reshape(experts, capacity, col_width)]
    reduce_scatter x1 -> x0, waiting for transfers between devices: 35.8 us -> none  [on_device(): lax.psum_scatter(partial_out, 'mp', scatter_dimension=1, tiled=True)]
    all_to_all x1, waiting for transfers between devices: 7.4 us -> 0.01 us  [on_device(): lax.all_to_all(back_rows, 'expert', split_axis=0, concat_axis=0, tiled=True)]
    concatenate x0 -> x5, local copies, waits for them, and re-layouts: none -> 6.68 us  [the longest x4 4.28 us: update(): jnp.concatenate([mlp_in[0], mlp_in[1] * scale, mlp_in[2], -mlp_bias, mlp_...]
  transfers between devices with their start and end apart: 3 -> 4, of which waited for: 2 -> 0; matrix products, arithmetic and copies ran while one was open for 11% -> 17% of each run, Pallas kernels for 0% -> 47%
where the time goes in v1:
time: 204 us; the launch traced here: 203 us
  Pallas kernels  131 us (64%)
  matrix products  29.4 us (14%)
  local copies, waits for them, and re-layouts  18.6 us (9%)
  other arithmetic  12.2 us (6%)
  starting transfers between devices  8.12 us (4%)
  between operations  3.71 us (2%)
    pallas_call x4, Pallas kernels, update(): pl.pallas_call(functools.partial(update_kernel, units, chunk), grid=(step...  65.2 us
    pallas_call x1, Pallas kernels, dispatch(): pl.pallas_call(functools.partial(dispatch_kernel, n, groups, colw), out_s...  35.3 us
    pallas_call x1, Pallas kernels, sum_experts(): pl.pallas_call(functools.partial(gather_experts_kernel, n), out_shape=jax...  17.3 us
    pallas_call x1, Pallas kernels, gather_all(): pl.pallas_call(functools.partial(gather_all_kernel, n, groups), out_shape...  13.3 us
    dot_general x1, matrix products, on_device(): jnp.einsum('sd,sf->df', rows_x, d_gate, preferred_element_type=jnp.float32)  8.59 us
    all_to_all x1, starting transfers between devices, on_device(): lax.all_to_all(back_rows, 'expert', split_axis=0, concat_axis=0, tiled=True)  5.22 us
    dot_general x1, matrix products, on_device(): jnp.einsum('sd,sf->df', rows_x, d_up, preferred_element_type=jnp.float32)  4.47 us
    concatenate x4, local copies, waits for them, and re-layouts, update(): jnp.concatenate([mlp_in[0], mlp_in[1] * scale, mlp_in[2], -mlp_bias, mlp_...  4.28 us
  transfers between devices with their start and end apart: 4, of which 0 were waited for; matrix products, arithmetic and copies ran while one was open for 17% of the time, Pallas kernels for 47%

profile of v1, /device:TPU:0, one launch (start us, length us, event | category | flops | bytes accessed | tf_op | source)
XLA Modules:
  0.0 203.2 jit_solution(3929069541963766548)
XLA Ops:
  0.6 0.0 copy-start
  0.7 0.7 convert_convert_fusion
  1.4 0.8 copy.20
  2.2 0.1 eq.62
  2.4 0.1 eq.58
  2.5 1.3 fusion.63
  3.8 0.7 fusion.42
  4.6 1.1 reduce-window.6
  5.7 0.2 slice_reduce_fusion
  6.0 0.1 fusion.45
  6.1 0.1 eq.66
  6.2 0.1 copy.22
  6.4 0.9 dynamic-slice_convert_fusion
  7.3 0.1 convert_reduce_fusion
  7.4 0.3 fusion.21
  7.7 0.5 fusion.18
  8.2 0.9 pad_maximum_fusion.send_ref
  9.2 35.3 %dispatch.1 = bf16[2,8,96,1024]{3,2,1,0:T(8,128)(2,1)} custom-call(bf16[2,8,96,256]{3,2,1,0:T(8,128)(2,1)} %pad_maximum_fusion.send_ref), custom_call_target="tpu_custom_call" | custom-call | tf_op jit(solution)/shard_map/dispatch/pallas_call | solution.py:123
  44.5 2.4 %fusion.60 = (bf16[1,8,96,1024]{3,2,1,0:T(8,128)(2,1)S(1)}, bf16[1,8,96,1024]{3,2,1,0:T(8,128)(2,1)S(1)}) fusion(bf16[2,8,96,1024]{3,2,1,0:T(8,128)(2,1)} %dispatch.1), kind=kLoop, calls=%fused_computation.92 | loop fusion | bytes 6291456 | tf_op jit(solution)/shard_map/slice | solution.py:380
  46.9 0.0 copy-start.6
  46.9 0.1 copy-done.1
  46.9 1.8 fusion.55
  48.7 0.8 copy-done.2
  49.5 1.8 fusion.53
  51.4 0.7 copy-done.3
  52.0 3.5 %multiply_reduce_fusion.3 = (f32[768]{0:T(1024)S(1)}, bf16[768,896]{1,0:T(8,128)(2,1)S(1)}, f32[768,896]{1,0:T(8,128)}) fusion(f32[768,896]{1,0:T(8,128)S(1)} %fusion.53, f32[768,896]{1,0:T(8,128)S(1)} %fusion.55, bf16[768,1024]{1,0:T(8,128)(2,1)S(1)} %bitcast.104, bf16[1,896,1024]{2,1,0:T(8,128)(2,1)S(1)} %copy-done.3), kind=kOutput, calls=%fused_computation.5 | convolution fusion | flops 1415478528 | bytes 13044736 | tf_op jit(solution)/shard_map/sd,fd->sf/dot_general | solution.py:402
  55.6 1.1 copy-done.21
  56.6 1.8 convolution_convert_fusion
  58.4 0.2 constant_dynamic-slice_fusion.3
  58.6 0.4 collective-permute-start
  59.0 1.4 collective-permute-start.2
  60.4 1.1 collective-permute-start.1
  61.5 8.6 %multiply_reduce_fusion.2 = (f32[]{:T(128)}, f32[1024,896]{1,0:T(8,128)}) fusion(bf16[768,1024]{1,0:T(8,128)(2,1)} %bitcast.108, f32[768,896]{1,0:T(8,128)} %copy-done.18, f32[768,896]{1,0:T(8,128)} %get-tuple-element.25, f32[768,896]{1,0:T(8,128)} %copy-done.20), kind=kOutput, calls=%fused_computation.2 | convolution fusion | flops 1418002432 | bytes 13500420 | tf_op jit(solution)/shard_map/sd,sf->df/dot_general | solution.py:408
  70.1 4.5 %multiply_reduce_fusion.1 = (f32[]{:T(128)}, f32[1024,896]{1,0:T(8,128)}) fusion(bf16[768,1024]{1,0:T(8,128)(2,1)S(1)} %bitcast.109, f32[768,896]{1,0:T(8,128)S(1)} %copy-done.23, f32[768,896]{1,0:T(8,128)S(1)} %copy-done.19), kind=kOutput, calls=%fused_computation.1 | convolution fusion | flops 1415249920 | bytes 10747908 | tf_op jit(solution)/shard_map/sd,sf->df/dot_general | solution.py:409
  74.6 4.2 %multiply_reduce_fusion = (f32[]{:T(128)}, f32[896,1024]{1,0:T(8,128)}) fusion(bf16[768,896]{1,0:T(8,128)(2,1)S(1)} %copy-done.22, bf16[768,1024]{1,0:T(8,128)(2,1)S(1)} %bitcast.105), kind=kOutput, calls=%fused_computation | convolution fusion | flops 1411121152 | bytes 6619140 | tf_op jit(solution)/shard_map/sf,sd->fd/dot_general | solution.py:401
  78.8 0.6 multiply_bitcast_fusion
  79.4 2.4 %concatenate.15 = f32[1024]{0:T(1024)} concatenate(f32[768]{0:T(1024)S(1)} %get-tuple-element.7, f32[1]{0:T(128)} %bitcast.24, f32[1]{0:T(128)} %bitcast.25, f32[1]{0:T(128)} %bitcast.26, f32[253]{0:T(256)S(1)} %broadcast_in_dim.20), dimensions={0} | concatenate | bytes 8192 | tf_op jit(solution)/shard_map/concatenate | solution.py:420
  81.8 13.3 %gather_all.1 = f32[32,8,128]{2,1,0:T(8,128)} custom-call(f32[8,128]{1,0:T(8,128)} %bitcast.112), custom_call_target="tpu_custom_call" | custom-call | tf_op jit(solution)/shard_map/gather_all/pallas_call | solution.py:187
  95.1 0.9 reshape.127
  96.1 0.1 reduce_sum.155
  96.2 0.7 fusion.62
  96.9 1.3 multiply_reduce_fusion.5
  98.2 0.1 constant_dynamic-slice_fusion
  100.2 1.4 concatenate.17
  101.6 1.4 concatenate.16
  103.0 0.4 fusion.1
  103.4 0.7 subtract_multiply_fusion
  104.1 2.2 %add_convert_fusion = bf16[768,256]{1,0:T(8,128)(2,1)} fusion(bf16[768,256]{1,0:T(8,128)(2,1)} %collective-permute-done.2, bf16[768,256]{1,0:T(8,128)(2,1)} %collective-permute-done.1, bf16[768,256]{1,0:T(8,128)(2,1)} %collective-permute-done, bf16[768,1024]{1,0:T(8,128)(2,1)S(1)} %convolution_convert_fusion, s32[]{:T(128)S(6)} %select_n.17), kind=kLoop, calls=%fused_computation.27 | loop fusion | flops 1572864 | bytes 1966084 | tf_op jit(solution)/shard_map/convert_element_type | solution.py:398
  106.3 5.2 %all-to-all-start = ((bf16[8,96,256]{2,1,0:T(8,128)(2,1)}), bf16[8,96,256]{2,1,0:T(8,128)(2,1)S(1)}, u32[]{:S(2)}, u32[]{:S(2)}) async-start(bf16[8,96,256]{2,1,0:T(8,128)(2,1)} %bitcast.13), calls=%async_computation | async-start | bytes 786432 | tf_op jit(solution)/shard_map/all_to_all | solution.py:399
  111.6 0.8 fusion.64.x_ref
  112.4 17.3 %sum_experts.1.g_ref = f32[8,1024]{1,0:T(8,128)} custom-call(f32[8,1024]{1,0:T(8,128)} %fusion.64.x_ref), custom_call_target="tpu_custom_call" | custom-call | tf_op jit(solution)/shard_map/sum_experts/pallas_call | solution.py:249
  129.7 1.4 multiply_reduce_fusion.4
  131.8 0.7 concatenate.19
  132.5 0.7 concatenate.18
  133.3 0.9 broadcast_in_dim.29.coef_ref
  134.1 1.9 update.7
  136.0 0.9 broadcast_in_dim.22.coef_ref
  136.9 21.0 %update.4 = bf16[1024,896]{1,0:T(8,128)(2,1)} custom-call(f32[82,8,128]{2,1,0:T(8,128)} %broadcast_in_dim.22.coef_ref, f32[1024,896]{1,0:T(8,128)} %get-tuple-element.27.g_ref, bf16[1024,896]{1,0:T(8,128)(2,1)} %bitcast.98), custom_call_target="tpu_custom_call" | custom-call | flops 132120576 | bytes 7340032 | tf_op jit(solution)/shard_map/update/pallas_call | solution.py:309
  157.9 0.9 broadcast_in_dim.24.coef_ref
  158.8 21.0 %update.5 = bf16[1024,896]{1,0:T(8,128)(2,1)} custom-call(f32[82,8,128]{2,1,0:T(8,128)} %broadcast_in_dim.24.coef_ref, f32[1024,896]{1,0:T(8,128)} %get-tuple-element.29.g_ref, bf16[1024,896]{1,0:T(8,128)(2,1)} %bitcast.99), custom_call_target="tpu_custom_call" | custom-call | flops 132120576 | bytes 7340032 | tf_op jit(solution)/shard_map/update/pallas_call | solution.py:309
  179.8 0.9 broadcast_in_dim.26.coef_ref
  180.7 21.3 %update.6 = bf16[896,1024]{1,0:T(8,128)(2,1)} custom-call(f32[82,8,128]{2,1,0:T(8,128)} %broadcast_in_dim.26.coef_ref, f32[896,1024]{1,0:T(8,128)} %get-tuple-element.31.g_ref, bf16[896,1024]{1,0:T(8,128)(2,1)} %bitcast.100), custom_call_target="tpu_custom_call" | custom-call | flops 132120576 | bytes 7340032 | tf_op jit(solution)/shard_map/update/pallas_call | solution.py:309
  202.0 0.4 fusion.15
  202.4 0.8 fusion.32
  (57 shorter events, 0.3 us)
Async XLA Ops:
  0.6 6.8 %copy-start = (bf16[256,1024]{1,0:T(8,128)(2,1)S(1)}, bf16[256,1024]{1,0:T(8,128)(2,1)}, u32[]{:S(2)}) copy-start(bf16[256,1024]{1,0:T(8,128)(2,1)} %param.10) | copy-start | bytes 1572868
  4.5 1.2 copy-start.12
  4.6 4.6 %copy-start.13 = (f32[256,2]{0,1:T(2,128)}, f32[256,2]{0,1:T(2,128)S(1)}, u32[]{:S(2)}) copy-start(f32[256,2]{0,1:T(2,128)S(1)} %multiply_divide_fusion) | copy-start | bytes 6148
  44.5 2.4 %copy-start.1 = (bf16[1,1024,896]{2,1,0:T(8,128)(2,1)S(1)}, bf16[1,1024,896]{2,1,0:T(8,128)(2,1)}, u32[]{:S(2)}) copy-start(bf16[1,1024,896]{2,1,0:T(8,128)(2,1)} %param.14) | copy-start | bytes 5505028
  46.9 1.9 copy-start.6
  46.9 4.5 %copy-start.4 = (bf16[1,8,96,1024]{3,2,1,0:T(8,128)(2,1)}, bf16[1,8,96,1024]{3,2,1,0:T(8,128)(2,1)S(1)}, u32[]{:S(2)}) copy-start(bf16[1,8,96,1024]{3,2,1,0:T(8,128)(2,1)S(1)} %get-tuple-element.10) | copy-start | bytes 4718596
  46.9 2.6 %copy-start.2 = (bf16[1,1024,896]{2,1,0:T(8,128)(2,1)S(1)}, bf16[1,1024,896]{2,1,0:T(8,128)(2,1)}, u32[]{:S(2)}) copy-start(bf16[1,1024,896]{2,1,0:T(8,128)(2,1)} %param.15) | copy-start | bytes 5505028
  49.5 1.8 copy-start.18
  49.5 2.5 %copy-start.3 = (bf16[1,896,1024]{2,1,0:T(8,128)(2,1)S(1)}, bf16[1,896,1024]{2,1,0:T(8,128)(2,1)}, u32[]{:S(2)}) copy-start(bf16[1,896,1024]{2,1,0:T(8,128)(2,1)} %param.16) | copy-start | bytes 5505028
  51.3 4.2 %copy-start.20 = (f32[768,896]{1,0:T(8,128)}, f32[768,896]{1,0:T(8,128)S(1)}, u32[]{:S(2)}) copy-start(f32[768,896]{1,0:T(8,128)S(1)} %fusion.53) | copy-start | bytes 8257540
  55.6 1.1 copy-start.21
  58.6 45.5 %collective-permute-start = (bf16[768,256]{1,0:T(8,128)(2,1)S(1)}, bf16[768,256]{1,0:T(8,128)(2,1)}, u32[]{:S(2)}, u32[]{:S(2)}) collective-permute-start(bf16[768,256]{1,0:T(8,128)(2,1)S(1)} %get-tuple-element.11), channel_id=1, source_target_pairs={{0,1},{1,2},{2,3},{3,0},{4,5},{5,6},{6,7},{7,4},{8,9},{9,10},{10,1... | collective-permute-start | bytes 1179656 | tf_op jit(solution)/shard_map/ppermute | solution.py:396
  59.0 45.1 %collective-permute-start.2 = (bf16[768,256]{1,0:T(8,128)(2,1)S(1)}, bf16[768,256]{1,0:T(8,128)(2,1)}, u32[]{:S(2)}, u32[]{:S(2)}) collective-permute-start(bf16[768,256]{1,0:T(8,128)(2,1)S(1)} %get-tuple-element.12), channel_id=1, source_target_pairs={{0,3},{1,0},{2,1},{3,2},{4,7},{5,4},{6,5},{7,6},{8,11},{9,8},{10,9... | collective-permute-start | bytes 1179656 | tf_op jit(solution)/shard_map/ppermute | solution.py:396
  60.4 43.7 %collective-permute-start.1 = (bf16[768,256]{1,0:T(8,128)(2,1)S(1)}, bf16[768,256]{1,0:T(8,128)(2,1)}, u32[]{:S(2)}, u32[]{:S(2)}) collective-permute-start(bf16[768,256]{1,0:T(8,128)(2,1)S(1)} %get-tuple-element.13), channel_id=1, source_target_pairs={{0,2},{1,3},{2,0},{3,1},{4,6},{5,7},{6,4},{7,5},{8,10},{9,11},{10,... | collective-permute-start | bytes 1179656 | tf_op jit(solution)/shard_map/ppermute | solution.py:396
  61.5 8.6 %copy-start.7 = (bf16[1,8,96,1024]{3,2,1,0:T(8,128)(2,1)S(1)}, bf16[1,8,96,1024]{3,2,1,0:T(8,128)(2,1)}, u32[]{:S(2)}) copy-start(bf16[1,8,96,1024]{3,2,1,0:T(8,128)(2,1)} %copy-done.6) | copy-start | bytes 4718596
  61.5 8.6 %copy-start.19 = (f32[768,896]{1,0:T(8,128)S(1)}, f32[768,896]{1,0:T(8,128)}, u32[]{:S(2)}) copy-start(f32[768,896]{1,0:T(8,128)} %copy-done.18) | copy-start | bytes 8257540
  61.5 8.6 %copy-start.23 = (f32[768,896]{1,0:T(8,128)S(1)}, f32[768,896]{1,0:T(8,128)}, u32[]{:S(2)}) copy-start(f32[768,896]{1,0:T(8,128)} %get-tuple-element.25) | copy-start | bytes 8257540
  70.1 4.5 %copy-start.5 = (bf16[1,8,96,1024]{3,2,1,0:T(8,128)(2,1)S(1)}, bf16[1,8,96,1024]{3,2,1,0:T(8,128)(2,1)}, u32[]{:S(2)}) copy-start(bf16[1,8,96,1024]{3,2,1,0:T(8,128)(2,1)} %copy-done.4) | copy-start | bytes 4718596
  70.1 4.5 %copy-start.22 = (bf16[768,896]{1,0:T(8,128)(2,1)S(1)}, bf16[768,896]{1,0:T(8,128)(2,1)}, u32[]{:S(2)}) copy-start(bf16[768,896]{1,0:T(8,128)(2,1)} %copy-done.21) | copy-start | bytes 4128772
  74.6 4.2 %copy-start.17 = (f32[3,16]{1,0:T(4,128)S(1)}, f32[3,16]{1,0:T(4,128)}, u32[]{:S(2)}) copy-start(f32[3,16]{1,0:T(4,128)} %param.17) | copy-start | bytes 580
  78.8 32.8 %copy-start.8 = (s32[256,2]{0,1:T(2,128)S(1)}, s32[256,2]{0,1:T(2,128)}, u32[]{:S(2)}) copy-start(s32[256,2]{0,1:T(2,128)} %param.12) | copy-start | bytes 6148
  96.1 35.6 %copy-start.9 = (f32[16]{0:T(128)S(1)}, f32[16]{0:T(128)}, u32[]{:S(2)}) copy-start(f32[16]{0:T(128)} %get-tuple-element.15) | copy-start | bytes 196
  96.2 35.6 %copy-start.10 = (f32[16]{0:T(128)S(1)}, f32[16]{0:T(128)}, u32[]{:S(2)}) copy-start(f32[16]{0:T(128)} %get-tuple-element.16) | copy-start | bytes 196
  96.2 35.6 %copy-start.11 = (f32[16]{0:T(128)S(1)}, f32[16]{0:T(128)}, u32[]{:S(2)}) copy-start(f32[16]{0:T(128)} %param.19) | copy-start | bytes 196
  96.2 35.6 %copy-start.15 = (f32[16]{0:T(128)S(1)}, f32[16]{0:T(128)}, u32[]{:S(2)}) copy-start(f32[16]{0:T(128)} %get-tuple-element.17) | copy-start | bytes 196
  96.2 36.3 %copy-start.16 = (f32[16]{0:T(128)S(1)}, f32[16]{0:T(128)}, u32[]{:S(2)}) copy-start(f32[16]{0:T(128)} %get-tuple-element.14) | copy-start | bytes 196
  106.3 95.7 %all-to-all-start = ((bf16[8,96,256]{2,1,0:T(8,128)(2,1)}), bf16[8,96,256]{2,1,0:T(8,128)(2,1)S(1)}, u32[]{:S(2)}, u32[]{:S(2)}) async-start(bf16[8,96,256]{2,1,0:T(8,128)(2,1)} %bitcast.13), calls=%async_computation | async-start | bytes 786432 | tf_op jit(solution)/shard_map/all_to_all | solution.py:399
  180.7 21.3 %copy-start.14 = (f32[256,2]{0,1:T(2,128)S(1)}, f32[256,2]{0,1:T(2,128)}, u32[]{:S(2)}) copy-start(f32[256,2]{0,1:T(2,128)} %copy-done.13) | copy-start | bytes 6148

commit v2 on v1

--- a/solution.py
+++ b/solution.py
@@ -8,6 +8,7 @@
 from jax.sharding import PartitionSpec as P
 
 EPSILON = 1e-06
+CHUNK = 128
 MESH = pl.DeviceIdType.MESH
 
 
@@ -141,130 +142,99 @@
     )(send)
 
 
-def gather_all_kernel(n, groups, x_ref, out_ref, loc, ss, rs):
-    total = n * groups
-    me = lax.axis_index("expert") * groups + lax.axis_index("mp")
+def gather_sums_kernel(n, groups, x_ref, out_ref, parts, mine, ms, mr, es, er):
+    me = lax.axis_index("expert")
+    col = lax.axis_index("mp")
     barrier = pltpu.get_barrier_semaphore()
 
-    def place(i):
-        peer = lax.rem(me + i, total)
-        return (peer // groups, lax.rem(peer, groups))
+    def greet_mp(i, _):
+        pl.semaphore_signal(
+            barrier, inc=1, device_id=(me, lax.rem(col + i, groups)), device_id_type=MESH
+        )
+        return 0
 
     def greet(i, _):
-        pl.semaphore_signal(barrier, inc=1, device_id=place(i), device_id_type=MESH)
-        return 0
-
-    own = pltpu.make_async_copy(x_ref, out_ref.at[me], loc)
-    own.start()
-    lax.fori_loop(1, total, greet, 0)
-    pl.semaphore_wait(barrier, total - 1)
-
-    def copy(i):
+        pl.semaphore_signal(
+            barrier, inc=1, device_id=(lax.rem(me + i, n), col), device_id_type=MESH
+        )
+        return 0
+
+    lax.fori_loop(1, groups, greet_mp, 0)
+    lax.fori_loop(1, n, greet, 0)
+    parts[col] = x_ref[...]
+    pl.semaphore_wait(barrier, groups - 1 + n - 1)
+
+    def across(i):
         return pltpu.make_async_remote_copy(
             src_ref=x_ref,
+            dst_ref=parts.at[col],
+            send_sem=ms.at[i],
+            recv_sem=mr.at[i],
+            device_id=(me, lax.rem(col + i, groups)),
+            device_id_type=MESH,
+        )
+
+    def spread(i):
+        return pltpu.make_async_remote_copy(
+            src_ref=mine,
             dst_ref=out_ref.at[me],
-            send_sem=ss.at[i],
-            recv_sem=rs.at[i],
-            device_id=place(i),
+            send_sem=es.at[i],
+            recv_sem=er.at[i],
+            device_id=(lax.rem(me + i, n), col),
             device_id_type=MESH,
         )
 
+    def start_across(i, _):
+        across(i).start()
+        return 0
+
+    def finish_across(i, _):
+        across(i).wait()
+        return 0
+
     def start(i, _):
-        copy(i).start()
+        spread(i).start()
         return 0
 
     def finish(i, _):
-        copy(i).wait()
-        return 0
-
-    lax.fori_loop(1, total, start, 0)
-    own.wait()
-    lax.fori_loop(1, total, finish, 0)
-
-
-def gather_all(x, n, groups):
-    total = n * groups
+        spread(i).wait()
+        return 0
+
+    lax.fori_loop(1, groups, start_across, 0)
+    lax.fori_loop(1, groups, finish_across, 0)
+    total = parts[0]
+    for i in range(1, groups):
+        total = total + parts[i]
+    mine[...] = total
+    out_ref[me] = total
+    lax.fori_loop(1, n, start, 0)
+    lax.fori_loop(1, n, finish, 0)
+
+
+def gather_sums(x, n, groups):
+    dma = pltpu.SemaphoreType.DMA
     return pl.pallas_call(
-        functools.partial(gather_all_kernel, n, groups),
-        out_shape=jax.ShapeDtypeStruct((total,) + x.shape, x.dtype),
+        functools.partial(gather_sums_kernel, n, groups),
+        out_shape=jax.ShapeDtypeStruct((n,) + x.shape, x.dtype),
         in_specs=[pl.BlockSpec(memory_space=pltpu.VMEM)],
         out_specs=pl.BlockSpec(memory_space=pltpu.VMEM),
         scratch_shapes=[
-            pltpu.SemaphoreType.DMA,
-            pltpu.SemaphoreType.DMA((total,)),
-            pltpu.SemaphoreType.DMA((total,)),
+            pltpu.VMEM((groups,) + x.shape, x.dtype),
+            pltpu.VMEM(x.shape, x.dtype),
+            dma((groups,)),
+            dma((groups,)),
+            dma((n,)),
+            dma((n,)),
         ],
         compiler_params=pltpu.CompilerParams(collective_id=1, has_side_effects=True),
-        name="gather_all",
+        name="gather_sums",
     )(x)
 
 
-def gather_experts_kernel(n, x_ref, out_ref, buf, loc, ss, rs):
-    me = lax.axis_index("expert")
-    col = lax.axis_index("mp")
-    barrier = pltpu.get_barrier_semaphore()
-
-    def greet(i, _):
-        pl.semaphore_signal(
-            barrier, inc=1, device_id=(lax.rem(me + i, n), col), device_id_type=MESH
-        )
-        return 0
-
-    own = pltpu.make_async_copy(x_ref, buf.at[me], loc)
-    own.start()
-    lax.fori_loop(1, n, greet, 0)
-    pl.semaphore_wait(barrier, n - 1)
-
-    def copy(i):
-        return pltpu.make_async_remote_copy(
-            src_ref=x_ref,
-            dst_ref=buf.at[me],
-            send_sem=ss.at[i],
-            recv_sem=rs.at[i],
-            device_id=(lax.rem(me + i, n), col),
-            device_id_type=MESH,
-        )
-
-    def start(i, _):
-        copy(i).start()
-        return 0
-
-    def finish(i, _):
-        copy(i).wait()
-        return 0
-
-    lax.fori_loop(1, n, start, 0)
-    own.wait()
-    lax.fori_loop(1, n, finish, 0)
-    out_ref[...] = buf[0]
-
-    def add(i, _):
-        out_ref[...] += buf[i]
-        return 0
-
-    lax.fori_loop(1, n, add, 0)
-
-
-def sum_experts(x, n):
-    return pl.pallas_call(
-        functools.partial(gather_experts_kernel, n),
-        out_shape=jax.ShapeDtypeStruct(x.shape, x.dtype),
-        in_specs=[pl.BlockSpec(memory_space=pltpu.VMEM)],
-        out_specs=pl.BlockSpec(memory_space=pltpu.VMEM),
-        scratch_shapes=[
-            pltpu.VMEM((n,) + x.shape, x.dtype),
-            pltpu.SemaphoreType.DMA,
-            pltpu.SemaphoreType.DMA((n,)),
-            pltpu.SemaphoreType.DMA((n,)),
-        ],
-        compiler_params=pltpu.CompilerParams(collective_id=2, has_side_effects=True),
-        name="sum_experts",
-    )(x)
-
-
-def update_kernel(units, chunk, coef_ref, g_ref, w_ref, out_ref):
+def update_kernel(units, chunk, scale, inv_ref, coef_ref, g_ref, w_ref, out_ref):
     rows, width = g_ref.shape
     strips = width // 128
+    inv = inv_ref[0]
 
     def body(step, _):
         r = pl.ds(pl.multiple_of((step // strips) * chunk, chunk), chunk)
@@ -273,10 +243,10 @@
         def coef(i):
             return jnp.concatenate([coef_ref[i]] * (chunk // 8), axis=0)
 
-        f0 = g_ref[r, c] * coef(5 * units)
-        f1 = w_ref[r, c].astype(jnp.float32)
+        f0 = g_ref[r, c] * inv
+        f1 = w_ref[r, c].astype(jnp.float32) * scale
         f2 = jnp.tanh(f0)
-        acc = coef(5 * units + 1)
+        acc = coef(5 * units)
         for j in range(units):
             y = coef(j) * f0 + coef(units + j) * f1 + coef(2 * units + j) * f2
             acc = acc + coef(4 * units + j) * jnp.maximum(y, coef(3 * units + j))
@@ -286,41 +256,148 @@
     lax.fori_loop(0, (rows // chunk) * strips, body, 0)
 
 
-def update(g, w, scale, rms, mlp_in, mlp_bias, mlp_out):
-    units = mlp_bias.shape[0]
-    table = jnp.concatenate(
-        [
-            mlp_in[0],
-            mlp_in[1] * scale,
-            mlp_in[2],
-            -mlp_bias,
-            mlp_out,
-            (1.0 / rms)[None],
-            jnp.sum(mlp_out * mlp_bias)[None],
-        ]
-    )
-    table = jnp.broadcast_to(table[:, None, None], (table.shape[0], 8, 128))
+def update_send_kernel(
+    units, chunk, scale, n, inv_ref, coef_ref, g_ref, w_ref, part_ref, rows_ref, out_ref, total_ref, back_ref, parts, returned, outgoing, ls, ps, pr, qs, qr
+):
+    me = lax.axis_index("expert")
+    col = lax.axis_index("mp")
+    step = pl.program_id(0)
+
+    def part(i):
+        return pltpu.make_async_remote_copy(
+            src_ref=parts.at[me],
+            dst_ref=parts.at[me],
+            send_sem=ps.at[i],
+            recv_sem=pr.at[i],
+            device_id=(lax.rem(me + i, n), col),
+            device_id_type=MESH,
+        )
+
+    def back(i):
+        peer = lax.rem(me + i, n)
+        return pltpu.make_async_remote_copy(
+            src_ref=outgoing.at[peer],
+            dst_ref=returned.at[me],
+            send_sem=qs.at[i],
+            recv_sem=qr.at[i],
+            device_id=(peer, col),
+            device_id_type=MESH,
+        )
+
+    def own():
+        return (
+            pltpu.make_async_copy(part_ref, parts.at[me], ls.at[0]),
+            pltpu.make_async_copy(rows_ref.at[me], returned.at[me], ls.at[1]),
+            pltpu.make_async_copy(rows_ref, outgoing, ls.at[2]),
+        )
+
+    @pl.when(step == 0)
+    def _():
+        barrier = pltpu.get_barrier_semaphore()
+
+        def greet(i, _):
+            pl.semaphore_signal(
+                barrier, inc=1, device_id=(lax.rem(me + i, n), col), device_id_type=MESH
+            )
+            return 0
+
+        lax.fori_loop(1, n, greet, 0)
+        for copy in own():
+            copy.start()
+        for copy in own():
+            copy.wait()
+        pl.semaphore_wait(barrier, n - 1)
+
+        def start(i, _):
+            part(i).start()
+            back(i).start()
+            return 0
+
+        lax.fori_loop(1, n, start, 0)
+
+    update_kernel(units, chunk, scale, inv_ref, coef_ref, g_ref, w_ref, out_ref)
+
+    @pl.when(step == pl.num_programs(0) - 1)
+    def _():
+        def finish(i, _):
+            part(i).wait()
+            back(i).wait()
+            return 0
+
+        lax.fori_loop(1, n, finish, 0)
+        total_ref[...] = parts[0]
+
+        def add(i, _):
+            total_ref[...] += parts[i]
+            return 0
+
+        lax.fori_loop(1, n, add, 0)
+        back_ref[...] = returned[...]
+
+
+def network_table(mlp_in, mlp_bias, mlp_out):
+    rows = jnp.concatenate(
+        [mlp_in.reshape(-1), -mlp_bias, mlp_out, jnp.sum(mlp_out * mlp_bias)[None]]
+    )
+    return jnp.broadcast_to(rows[:, None, None], (rows.shape[0], 8, 128))
+
+
+def update(g, w, scale, rms, table, send=None):
+    units = table.shape[0] // 5
+    inv = (1.0 / rms).reshape(1)
     rows, width = g.shape
-    chunk = 64 if rows % 64 == 0 else rows
+    chunk = CHUNK if rows % CHUNK == 0 else rows
     steps = 4 if rows % (4 * chunk) == 0 else 2 if rows % (2 * chunk) == 0 else 1
-    if chunk < 64:
+    if chunk == rows:
         chunk = 8
     block = rows // steps
+    in_specs = [
+        pl.BlockSpec(memory_space=pltpu.SMEM),
+        pl.BlockSpec(table.shape, lambda i: (0, 0, 0)),
+        pl.BlockSpec((block, width), lambda i: (i, 0)),
+        pl.BlockSpec((block, width), lambda i: (i, 0)),
+    ]
+    out_shape = jax.ShapeDtypeStruct((rows, width), jnp.bfloat16)
+    out_spec = pl.BlockSpec((block, width), lambda i: (i, 0))
+    cost = pl.CostEstimate(
+        flops=rows * width * 9 * units, bytes_accessed=rows * width * 8, transcendentals=rows * width
+    )
+    if send is None:
+        return pl.pallas_call(
+            functools.partial(update_kernel, units, chunk, scale),
+            grid=(steps,),
+            out_shape=out_shape,
+            in_specs=in_specs,
+            out_specs=out_spec,
+            cost_estimate=cost,
+            name="update",
+        )(inv, table, g, w)
+    part, rows_back = send
+    n = rows_back.shape[0]
+    dma = pltpu.SemaphoreType.DMA
     return pl.pallas_call(
-        functools.partial(update_kernel, units, chunk),
+        functools.partial(update_send_kernel, units, chunk, scale, n),
         grid=(steps,),
-        out_shape=jax.ShapeDtypeStruct((rows, width), jnp.bfloat16),
-        in_specs=[
-            pl.BlockSpec(table.shape, lambda i: (0, 0, 0)),
-            pl.BlockSpec((block, width), lambda i: (i, 0)),
-            pl.BlockSpec((block, width), lambda i: (i, 0)),
-        ],
-        out_specs=pl.BlockSpec((block, width), lambda i: (i, 0)),
-        cost_estimate=pl.CostEstimate(
-            flops=rows * width * 9 * units, bytes_accessed=rows * width * 8, transcendentals=rows * width
+        out_shape=(
+            out_shape,
+            jax.ShapeDtypeStruct(part.shape, part.dtype),
+            jax.ShapeDtypeStruct(rows_back.shape, rows_back.dtype),
         ),
-        name="update",
-    )(table, g, w)
+        in_specs=in_specs + [pl.BlockSpec(memory_space=pl.ANY)] * 2,
+        out_specs=(
+            out_spec,
+            pl.BlockSpec(part.shape, lambda i: (0, 0)),
+            pl.BlockSpec(rows_back.shape, lambda i: (0, 0, 0)),
+        ),
+        scratch_shapes=[
+            pltpu.VMEM((n,) + part.shape, part.dtype),
+            pltpu.VMEM(rows_back.shape, rows_back.dtype),
+            pltpu.VMEM(rows_back.shape, rows_back.dtype),
+            dma((3,)), dma((n,)), dma((n,)), dma((n,)), dma((n,))],
+        cost_estimate=cost,
+        compiler_params=pltpu.CompilerParams(collective_id=2, has_side_effects=True),
+        name="update_send",
+    )(inv, table, g, w, part, rows_back)
 
 
 def route_tables(routes, experts, capacity):
@@ -389,6 +466,30 @@
     silu_gate = act_gate * sigmoid_gate
     hidden = (silu_gate * act_up).astype(jnp.bfloat16)
     partial_out = jnp.dot(hidden, w_down, preferred_element_type=jnp.float32).astype(jnp.bfloat16)
+    grad_down = jnp.einsum("sf,sd->fd", hidden, rows_dy, preferred_element_type=jnp.float32)
+    grad_hidden = jnp.einsum("sd,fd->sf", rows_dy, w_down, preferred_element_type=jnp.float32)
+    d_gate = (grad_hidden * act_up * sigmoid_gate * (1.0 + act_gate * (1.0 - sigmoid_gate))).astype(
+        jnp.bfloat16
+    )
+    d_up = (grad_hidden * silu_gate).astype(jnp.bfloat16)
+    d_gate, d_up = lax.optimization_barrier((d_gate, d_up))
+    inner = jnp.sum(grad_hidden * hidden.astype(jnp.float32), axis=1)
+    grad_gate = jnp.einsum("sd,sf->df", rows_x, d_gate, preferred_element_type=jnp.float32)
+    grad_up = jnp.einsum("sd,sf->df", rows_x, d_up, preferred_element_type=jnp.float32)
+
+    norms = jnp.stack(
+        [
+            jnp.sum(grad_gate * grad_gate),
+            jnp.sum(grad_up * grad_up),
+            jnp.sum(grad_down * grad_down),
+        ]
+    )
+    need = slots + 3
+    lines = -(-need // 1024) * 8
+    parcel = jnp.concatenate([inner, norms, jnp.zeros((lines * 128 - need,), jnp.float32)])
+    parcels = gather_sums(parcel.reshape(lines, 128), experts, groups)
+    parcels = parcels.reshape(experts, lines * 128)
+    partial_out, parcels = lax.optimization_barrier((partial_out, parcels))
     total_out = lax.dynamic_slice_in_dim(partial_out, col_start, col_width, 1).astype(jnp.float32)
     for shift in range(1, groups):
         target = lax.rem(mp + shift, groups)
@@ -396,47 +497,26 @@
         moved = lax.ppermute(piece, "mp", [(m, (m + shift) % groups) for m in range(groups)])
         total_out = total_out + moved.astype(jnp.float32)
     back_rows = total_out.astype(jnp.bfloat16).reshape(experts, capacity, col_width)
-    returned = lax.all_to_all(back_rows, "expert", split_axis=0, concat_axis=0, tiled=True)
-
-    grad_down = jnp.einsum("sf,sd->fd", hidden, rows_dy, preferred_element_type=jnp.float32)
-    grad_hidden = jnp.einsum("sd,fd->sf", rows_dy, w_down, preferred_element_type=jnp.float32)
-    d_gate = (grad_hidden * act_up * sigmoid_gate * (1.0 + act_gate * (1.0 - sigmoid_gate))).astype(
-        jnp.bfloat16
-    )
-    d_up = (grad_hidden * silu_gate).astype(jnp.bfloat16)
-    inner = jnp.sum(grad_hidden * hidden.astype(jnp.float32), axis=1)
-    grad_gate = jnp.einsum("sd,sf->df", rows_x, d_gate, preferred_element_type=jnp.float32)
-    grad_up = jnp.einsum("sd,sf->df", rows_x, d_up, preferred_element_type=jnp.float32)
-
-    norms = jnp.stack(
-        [
-            jnp.sum(grad_gate * grad_gate),
-            jnp.sum(grad_up * grad_up),
-            jnp.sum(grad_down * grad_down),
-        ]
-    )
-    need = slots + 3
-    lines = -(-need // 1024) * 8
-    parcel = jnp.concatenate([inner, norms, jnp.zeros((lines * 128 - need,), jnp.float32)])
-    parcels = gather_all(parcel.reshape(lines, 128), experts, groups)
-    parcels = jnp.sum(parcels.reshape(experts, groups, lines * 128), axis=1)
+
     norm_sums = jnp.sum(parcels[:, slots : slots + 3], axis=0)
     inner_own = lax.dynamic_slice(parcels, (0, me * capacity), (experts, capacity))
 
     total_count = experts * width * hidden_units
     rms = jnp.sqrt(norm_sums / total_count + EPSILON)
-    net = (mlp_in, mlp_bias, mlp_out)
-    gate_update = update(grad_gate, w_gate, width**0.5, rms[0], *net)[None]
-    up_update = update(grad_up, w_up, width**0.5, rms[1], *net)[None]
-    down_update = update(grad_down, w_down, hidden_units**0.5, rms[2], *net)[None]
+    table = network_table(mlp_in, mlp_bias, mlp_out)
+    up_update = update(grad_up, w_up, width**0.5, rms[1], table)[None]
+    down_update = update(grad_down, w_down, hidden_units**0.5, rms[2], table)[None]
 
     gated = jnp.sum(mover.astype(jnp.float32) * inner_own[None, None], axis=(2, 3))
     logit_grads = (gated - gates * jnp.sum(gated, axis=1, keepdims=True)) * (1.0 - sigmas)
     dense_grads = jnp.sum(logit_grads[:, :, None] * chosen, axis=1).astype(jnp.bfloat16)
     router_part = jnp.einsum("te,td->ed", dense_grads, tokens, preferred_element_type=jnp.float32)
-    router_grad = sum_experts(router_part, experts)
+    gate_update, router_grad, returned = update(
+        grad_gate, w_gate, width**0.5, rms[0], table, send=(router_part, back_rows)
+    )
+    gate_update = gate_update[None]
     router_rms = jnp.sqrt(jnp.sum(router_grad * router_grad) / (width * experts) + EPSILON)
-    router_update = update(router_grad, router_weight.T, width**0.5, router_rms, *net).T
+    router_update = update(router_grad, router_weight.T, width**0.5, router_rms, table).T
 
     routed = jnp.einsum("tkec,ecd->tkd", mover, returned, preferred_element_type=jnp.float32)
     mixed = (

time: 204 us -> 176 us (0.86)
  Pallas kernels: 131 us -> 117 us
  local copies, waits for them, and re-layouts: 18.6 us -> 11.4 us
  starting transfers between devices: 8.12 us -> 2.35 us
    pallas_call x6 -> x5, Pallas kernels: 95.9 us -> 81.5 us  [the longest x3 43.5 us: update(): pl.pallas_call(functools.partial(update_kernel, units, chunk, scale), gri...]
    all_to_all x1 -> x0, starting transfers between devices: 5.22 us -> none  [on_device(): lax.all_to_all(back_rows, 'expert', split_axis=0, concat_axis=0, tiled=True)]
    concatenate x4 -> x0, local copies, waits for them, and re-layouts: 4.28 us -> none  [update(): jnp.concatenate([mlp_in[0], mlp_in[1] * scale, mlp_in[2], -mlp_bias, mlp_...]
    dot_general x1, matrix products: 8.59 us -> 5.78 us  [on_device(): jnp.einsum('sd,sf->df', rows_x, d_gate, preferred_element_type=jnp.float32)]
    broadcast_in_dim x4 -> x1, local copies, waits for them, and re-layouts: 3.5 us -> 0.89 us  [network_table(): return jnp.broadcast_to(rows[:, None, None], (rows.shape[0], 8, 128))]
  transfers between devices with their start and end apart: 4 -> 3, of which waited for: 0 -> 0; matrix products, arithmetic and copies ran while one was open for 17% -> 2% of each run, Pallas kernels for 47% -> 24%
where the time goes in v2:
time: 176 us
  Pallas kernels  117 us (66%)
  matrix products  30.6 us (17%)
  local copies, waits for them, and re-layouts  11.4 us (6%)
  other arithmetic  11 us (6%)
  between operations  3.63 us (2%)
  starting transfers between devices  2.35 us (1%)
    pallas_call x3, Pallas kernels, update(): pl.pallas_call(functools.partial(update_kernel, units, chunk, scale), gri...  43.5 us
    pallas_call x1, Pallas kernels, dispatch(): pl.pallas_call(functools.partial(dispatch_kernel, n, groups, colw), out_s...  35.3 us
    pallas_call x1, Pallas kernels, update(): pl.pallas_call(functools.partial(update_send_kernel, units, chunk, scale,...  23.8 us
    pallas_call x1, Pallas kernels, gather_sums(): pl.pallas_call(functools.partial(gather_sums_kernel, n, groups), out_shap...  14.1 us
    dot_general x1, matrix products, on_device(): jnp.einsum('sd,sf->df', rows_x, d_up, preferred_element_type=jnp.float32)  5.79 us
    dot_general x1, matrix products, on_device(): jnp.einsum('sd,sf->df', rows_x, d_gate, preferred_element_type=jnp.float32)  5.78 us
    dot_general x1, matrix products, on_device(): jnp.einsum('sd,fd->sf', rows_dy, w_down, preferred_element_type=jnp.float32)  4.25 us
    dot_general x1, matrix products, on_device(): jnp.einsum('sf,sd->fd', hidden, rows_dy, preferred_element_type=jnp.float32)  4.04 us
  transfers between devices with their start and end apart: 3, of which 0 were waited for; matrix products, arithmetic and copies ran while one was open for 2% of the time, Pallas kernels for 24%

profile of v2, /device:TPU:0, one launch (start us, length us, event | category | flops | bytes accessed | tf_op | source)
XLA Modules:
  0.0 175.8 jit_solution(9543878704136905592)
XLA Ops:
  0.6 0.0 copy-start
  0.6 0.9 copy.20
  1.5 0.1 eq.62
  1.7 0.1 eq.58
  1.8 0.7 convert_convert_fusion
  2.5 1.1 reduce-window.6
  3.6 0.2 slice_reduce_fusion
  3.9 0.1 fusion.42
  4.0 0.1 eq.66
  4.2 0.1 copy.22
  4.3 1.3 fusion.59
  5.5 0.7 fusion.39
  6.3 0.9 dynamic-slice_convert_fusion
  7.2 0.1 convert_reduce_fusion
  7.4 0.0 copy-done
  7.4 0.3 fusion.19
  7.7 0.5 fusion.16
  8.2 0.9 pad_maximum_fusion.send_ref
  9.1 35.3 %dispatch.1 = bf16[2,8,96,1024]{3,2,1,0:T(8,128)(2,1)} custom-call(bf16[2,8,96,256]{3,2,1,0:T(8,128)(2,1)} %pad_maximum_fusion.send_ref), custom_call_target="tpu_custom_call" | custom-call | tf_op jit(solution)/shard_map/dispatch/pallas_call | solution.py:124
  44.4 0.0 copy-start.2
  44.4 2.5 %fusion.55 = (bf16[1,8,96,1024]{3,2,1,0:T(8,128)(2,1)S(1)}, bf16[1,8,96,1024]{3,2,1,0:T(8,128)(2,1)S(1)}) fusion(bf16[2,8,96,1024]{3,2,1,0:T(8,128)(2,1)} %dispatch.1), kind=kLoop, calls=%fused_computation.86 | loop fusion | bytes 6291456 | tf_op jit(solution)/shard_map/slice | solution.py:457
  46.9 0.0 copy-start.6
  46.9 0.0 copy-done.2
  46.9 0.0 copy-start.4
  46.9 1.8 %fusion.50 = f32[768,896]{1,0:T(8,128)S(1)} fusion(bf16[768,1024]{1,0:T(8,128)(2,1)S(1)} %bitcast.103, bf16[1,1024,896]{2,1,0:T(8,128)(2,1)S(1)} %copy-done.2), kind=kOutput, calls=%fused_computation.81 | convolution fusion | flops 1409286144 | bytes 6160384 | tf_op jit(solution)/shard_map/dot_general | solution.py:464
  48.7 0.3 copy-done.4
  49.0 1.8 %fusion.52 = f32[768,896]{1,0:T(8,128)S(1)} fusion(bf16[768,1024]{1,0:T(8,128)(2,1)S(1)} %bitcast.104, bf16[1,1024,896]{2,1,0:T(8,128)(2,1)S(1)} %copy-done.4), kind=kOutput, calls=%fused_computation.83 | convolution fusion | flops 1409286144 | bytes 6160384 | tf_op jit(solution)/shard_map/dot_general | solution.py:463
  50.8 0.0 copy-done.1
  50.8 4.3 %multiply_reduce_fusion.3 = (f32[768]{0:T(1024)S(1)}, bf16[768,896]{1,0:T(8,128)(2,1)S(1)}, bf16[768,896]{1,0:T(8,128)(2,1)}, bf16[768,896]{1,0:T(8,128)(2,1)}) fusion(f32[768,896]{1,0:T(8,128)S(1)} %fusion.50, f32[768,896]{1,0:T(8,128)S(1)} %fusion.52, bf16[768,1024]{1,0:T(8,128)(2,1)S(1)} %bitcast.107, bf16[1,896,1024]{2,1,0:T(8,128)(2,1)S(1)} %copy-done.1), kind=kOutput, calls=%fused_computation.5 | convolution fusion | flops 1421671680 | bytes 13044736 | tf_op jit(solution)/shard_map/sd,fd->sf/dot_general | solution.py:470
  55.1 4.0 %multiply_reduce_fusion = (f32[]{:T(128)}, f32[896,1024]{1,0:T(8,128)}) fusion(bf16[768,896]{1,0:T(8,128)(2,1)S(1)} %get-tuple-element.22, bf16[768,1024]{1,0:T(8,128)(2,1)S(1)} %bitcast.108), kind=kOutput, calls=%fused_computation | convolution fusion | flops 1411121152 | bytes 6619140 | tf_op jit(solution)/shard_map/sf,sd->fd/dot_general | solution.py:469
  59.1 2.9 %convolution_convert_fusion = bf16[768,1024]{1,0:T(8,128)(2,1)} fusion(bf16[768,896]{1,0:T(8,128)(2,1)S(1)} %get-tuple-element.22, bf16[1,896,1024]{2,1,0:T(8,128)(2,1)S(1)} %copy-done.1), kind=kOutput, calls=%fused_computation.17 | convolution fusion | flops 1410072576 | bytes 4784128 | tf_op jit(solution)/shard_map/dot_general | solution.py:468
  62.0 5.8 %multiply_reduce_fusion.1 = (f32[]{:T(128)}, f32[1024,896]{1,0:T(8,128)}) fusion(bf16[768,1024]{1,0:T(8,128)(2,1)S(1)} %bitcast.105, bf16[768,896]{1,0:T(8,128)(2,1)} %get-tuple-element.13), kind=kOutput, calls=%fused_computation.1 | convolution fusion | flops 1411121152 | bytes 6619140 | tf_op jit(solution)/shard_map/sd,sf->df/dot_general | solution.py:478
  67.8 5.8 %multiply_reduce_fusion.2 = (f32[]{:T(128)}, f32[1024,896]{1,0:T(8,128)}) fusion(bf16[768,1024]{1,0:T(8,128)(2,1)} %bitcast.106, bf16[768,896]{1,0:T(8,128)(2,1)S(1)} %copy-done.11), kind=kOutput, calls=%fused_computation.2 | convolution fusion | flops 1411121152 | bytes 6619140 | tf_op jit(solution)/shard_map/sd,sf->df/dot_general | solution.py:477
  73.6 2.5 %concatenate.6 = f32[1024]{0:T(1024)} concatenate(f32[768]{0:T(1024)S(1)} %get-tuple-element.21, f32[1]{0:T(128)} %bitcast.14, f32[1]{0:T(128)} %bitcast.15, f32[1]{0:T(128)} %bitcast.16, f32[253]{0:T(256)S(1)} %broadcast_in_dim.12), dimensions={0} | concatenate | bytes 8192 | tf_op jit(solution)/shard_map/concatenate | solution.py:489
  76.1 14.1 %gather_sums.1 = f32[8,8,128]{2,1,0:T(8,128)} custom-call(f32[8,128]{1,0:T(8,128)} %bitcast.114), custom_call_target="tpu_custom_call" | custom-call | tf_op jit(solution)/shard_map/gather_sums/pallas_call | solution.py:216
  90.3 0.8 copy.27
  91.1 0.9 constant_dynamic-slice_fusion.2
  92.0 0.0 collective-permute-start
  92.0 0.9 collective-permute-start.1
  92.9 1.5 collective-permute-start.2
  94.3 0.1 constant_dynamic-slice_fusion.3
  94.4 0.4 fusion.1
  94.8 0.6 fusion.57
  95.4 0.1 reshape.129
  95.5 0.0 copy-done.9
  95.5 0.0 copy-done.10
  95.5 0.6 fusion.58
  96.1 0.7 pad_maximum_fusion.1
  98.9 0.9 broadcast_in_dim.14.coef_ref
  99.8 21.6 %update.4 = bf16[896,1024]{1,0:T(8,128)(2,1)} custom-call(f32[1]{0:T(128)S(6)} %div.51.inv_ref, f32[81,8,128]{2,1,0:T(8,128)} %broadcast_in_dim.14.coef_ref, f32[896,1024]{1,0:T(8,128)} %get-tuple-element.42.g_ref, bf16[896,1024]{1,0:T(8,128)(2,1)} %bitcast.96), custom_call_target="tpu_custom_call" | custom-call | flops 132120576 | bytes 7340032 | tf_op jit(solution)/shard_map/update/pallas_call | solution.py:366
  121.4 20.1 %update.3 = bf16[1024,896]{1,0:T(8,128)(2,1)} custom-call(f32[1]{0:T(128)S(6)} %div.50.inv_ref, f32[81,8,128]{2,1,0:T(8,128)} %broadcast_in_dim.14.coef_ref, f32[1024,896]{1,0:T(8,128)} %get-tuple-element.40.g_ref, bf16[1024,896]{1,0:T(8,128)(2,1)} %bitcast.97), custom_call_target="tpu_custom_call" | custom-call | flops 132120576 | bytes 7340032 | tf_op jit(solution)/shard_map/update/pallas_call | solution.py:366
  141.4 0.0 copy-done.7
  141.5 0.8 fusion.60.part_ref
  142.3 0.0 collective-permute-done
  142.3 0.0 collective-permute-done.1
  142.3 0.0 collective-permute-done.2
  142.3 2.2 %add_convert_fusion = bf16[768,256]{1,0:T(8,128)(2,1)} fusion(bf16[768,256]{1,0:T(8,128)(2,1)} %collective-permute-done.2, bf16[768,256]{1,0:T(8,128)(2,1)} %collective-permute-done.1, bf16[768,256]{1,0:T(8,128)(2,1)} %collective-permute-done, bf16[768,1024]{1,0:T(8,128)(2,1)S(1)} %copy-done.5, s32[]{:T(128)S(6)} %select_n.17), kind=kLoop, calls=%fused_computation.25 | loop fusion | flops 1572864 | bytes 1966084 | tf_op jit(solution)/shard_map/convert_element_type | solution.py:499
  144.4 23.8 %update_send.1 = (bf16[1024,896]{1,0:T(8,128)(2,1)}, f32[8,1024]{1,0:T(8,128)}, bf16[8,96,256]{2,1,0:T(8,128)(2,1)}) custom-call(f32[1]{0:T(128)S(6)} %div.49.inv_ref, f32[81,8,128]{2,1,0:T(8,128)} %broadcast_in_dim.14.coef_ref, f32[1024,896]{1,0:T(8,128)} %get-tuple-element.38.g_ref, bf16[1024,896]{1,0:T(8,128)(2,1)} %bitcast.101, ...), custom_call_target="tpu_custom_call" | custom-call | flops 132120576 | bytes 7340032 | tf_op jit(solution)/shard_map/update_send/pallas_call | solution.py:378
  168.3 0.0 copy-start.3
  168.3 1.5 multiply_reduce_fusion.4
  170.5 1.4 fusion.13
  171.9 1.9 %update.5 = bf16[8,1024]{1,0:T(8,128)(2,1)} custom-call(f32[1]{0:T(128)} %bitcast.29.inv_ref, f32[81,8,128]{2,1,0:T(8,128)} %broadcast_in_dim.14.coef_ref, f32[8,1024]{1,0:T(8,128)} %get-tuple-element.18.g_ref, bf16[8,1024]{1,0:T(8,128)(2,1)} %bitcast.110), custom_call_target="tpu_custom_call" | custom-call | flops 1179648 | bytes 65536 | tf_op jit(solution)/shard_map/update/pallas_call | solution.py:366
  173.8 0.8 fusion.29
  174.6 1.2 copy.29
  (24 shorter events, 0.2 us)
Async XLA Ops:
  0.6 6.8 %copy-start = (bf16[256,1024]{1,0:T(8,128)(2,1)S(1)}, bf16[256,1024]{1,0:T(8,128)(2,1)}, u32[]{:S(2)}) copy-start(bf16[256,1024]{1,0:T(8,128)(2,1)} %param.10) | copy-start | bytes 1572868
  44.4 2.5 %copy-start.2 = (bf16[1,1024,896]{2,1,0:T(8,128)(2,1)S(1)}, bf16[1,1024,896]{2,1,0:T(8,128)(2,1)}, u32[]{:S(2)}) copy-start(bf16[1,1024,896]{2,1,0:T(8,128)(2,1)} %param.15) | copy-start | bytes 5505028
  46.9 15.1 %copy-start.6 = (bf16[1,8,96,1024]{3,2,1,0:T(8,128)(2,1)}, bf16[1,8,96,1024]{3,2,1,0:T(8,128)(2,1)S(1)}, u32[]{:S(2)}) copy-start(bf16[1,8,96,1024]{3,2,1,0:T(8,128)(2,1)S(1)} %get-tuple-element.25) | copy-start | bytes 4718596
  46.9 2.1 %copy-start.4 = (bf16[1,1024,896]{2,1,0:T(8,128)(2,1)S(1)}, bf16[1,1024,896]{2,1,0:T(8,128)(2,1)}, u32[]{:S(2)}) copy-start(bf16[1,1024,896]{2,1,0:T(8,128)(2,1)} %param.14) | copy-start | bytes 5505028
  49.0 1.8 %copy-start.1 = (bf16[1,896,1024]{2,1,0:T(8,128)(2,1)S(1)}, bf16[1,896,1024]{2,1,0:T(8,128)(2,1)}, u32[]{:S(2)}) copy-start(bf16[1,896,1024]{2,1,0:T(8,128)(2,1)} %param.16) | copy-start | bytes 5505028
  62.0 5.8 %copy-start.11 = (bf16[768,896]{1,0:T(8,128)(2,1)S(1)}, bf16[768,896]{1,0:T(8,128)(2,1)}, u32[]{:S(2)}) copy-start(bf16[768,896]{1,0:T(8,128)(2,1)} %get-tuple-element.12) | copy-start | bytes 4128772
  67.8 23.2 %copy-start.5 = (bf16[768,1024]{1,0:T(8,128)(2,1)S(1)}, bf16[768,1024]{1,0:T(8,128)(2,1)}, u32[]{:S(2)}) copy-start(bf16[768,1024]{1,0:T(8,128)(2,1)} %convolution_convert_fusion) | copy-start | bytes 4718596
  73.6 21.8 %copy-start.8 = (f32[3,16]{1,0:T(4,128)S(1)}, f32[3,16]{1,0:T(4,128)}, u32[]{:S(2)}) copy-start(f32[3,16]{1,0:T(4,128)} %param.17) | copy-start | bytes 580
  73.6 21.9 %copy-start.9 = (f32[16]{0:T(128)S(1)}, f32[16]{0:T(128)}, u32[]{:S(2)}) copy-start(f32[16]{0:T(128)} %param.19) | copy-start | bytes 196
  73.6 21.9 %copy-start.10 = (f32[16]{0:T(128)S(1)}, f32[16]{0:T(128)}, u32[]{:S(2)}) copy-start(f32[16]{0:T(128)} %param.18) | copy-start | bytes 196
  92.0 50.3 %collective-permute-start = (bf16[768,256]{1,0:T(8,128)(2,1)}, bf16[768,256]{1,0:T(8,128)(2,1)}, u32[]{:S(2)}, u32[]{:S(2)}) collective-permute-start(bf16[768,256]{1,0:T(8,128)(2,1)} %get-tuple-element.27), channel_id=1, source_target_pairs={{0,1},{1,2},{2,3},{3,0},{4,5},{5,6},{6,7},{7,4},{8,9},{9,10},{10,1... | collective-permute-start | bytes 1179656 | tf_op jit(solution)/shard_map/ppermute | solution.py:497
  92.0 50.3 %collective-permute-start.1 = (bf16[768,256]{1,0:T(8,128)(2,1)S(1)}, bf16[768,256]{1,0:T(8,128)(2,1)}, u32[]{:S(2)}, u32[]{:S(2)}) collective-permute-start(bf16[768,256]{1,0:T(8,128)(2,1)S(1)} %get-tuple-element.29), channel_id=1, source_target_pairs={{0,2},{1,3},{2,0},{3,1},{4,6},{5,7},{6,4},{7,5},{8,10},{9,11},{10,... | collective-permute-start | bytes 1179656 | tf_op jit(solution)/shard_map/ppermute | solution.py:497
  92.9 49.4 %collective-permute-start.2 = (bf16[768,256]{1,0:T(8,128)(2,1)S(1)}, bf16[768,256]{1,0:T(8,128)(2,1)}, u32[]{:S(2)}, u32[]{:S(2)}) collective-permute-start(bf16[768,256]{1,0:T(8,128)(2,1)S(1)} %get-tuple-element.28), channel_id=1, source_target_pairs={{0,3},{1,0},{2,1},{3,2},{4,7},{5,4},{6,5},{7,6},{8,11},{9,8},{10,9... | collective-permute-start | bytes 1179656 | tf_op jit(solution)/shard_map/ppermute | solution.py:497
  121.4 20.1 %copy-start.7 = (s32[256,2]{0,1:T(2,128)S(1)}, s32[256,2]{0,1:T(2,128)}, u32[]{:S(2)}) copy-start(s32[256,2]{0,1:T(2,128)} %param.12) | copy-start | bytes 6148
  168.3 6.3 %copy-start.3 = (bf16[1024,896]{1,0:T(8,128)(2,1)S(1)}, bf16[1024,896]{1,0:T(8,128)(2,1)}, u32[]{:S(2)}) copy-start(bf16[1024,896]{1,0:T(8,128)(2,1)} %get-tuple-element.17) | copy-start | bytes 5505028
